TPU v7x, 64 devices: a 2x2x8 block of a 4x4x8 slice. The times are simulated.
64 devices in a mesh: data: 4 (over x, y), model: 16 (over z, core).
Axes of the slice: x: 2, y: 2, z: 8, core: 2. Of those that a mesh axis runs over, the one named last changes fastest.
The devices are a block of a 4x4x8 slice.
Arguments:
- images: bfloat16 [12, 256, 256, 64], P('data', None, None, 'model'), parts along dimension 0
- w_conv1: bfloat16 [3, 3, 64, 128], P(None, None, 'model')
- b_conv1: float32 [128], replicated
- w_conv2: bfloat16 [3, 3, 128, 128], replicated
- b_conv2: float32 [128], replicated
- w_short: bfloat16 [64, 128], P('model')
Outputs:
- output: float32 [12, 256, 256, 128], P('data', 'model'), parts along dimension 0
There are 4 independent parts. A program takes and returns all parts, laid end to end along the dimension named above; an argument that names none is the same for every part.
All inputs are finite; a program needn't handle non-finite values.
Results may differ from a plain program's by a relative error of at most 0.00609846.
Values are sent between devices in bfloat16 or wider.
A program may use at most 768 MiB of HBM per device.

v0:
```python
import jax
import jax.numpy as jnp
from jax import lax
from jax.sharding import PartitionSpec as P, NamedSharding

CONV_LAYOUT = ('NHWC', 'HWIO', 'NHWC')


def solution(mesh):
    groups = mesh.shape['model']

    def local_step(images, w_conv1, b_conv1, w_conv2, b_conv2, w_short):
        num_images, height, img_width, _ = images.shape
        tile_rows = height // groups
        my_index = lax.axis_index('model')
        part_sum = lax.conv_general_dilated(images, w_conv1, (1, 1), 'SAME', dimension_numbers=CONV_LAYOUT, preferred_element_type=jnp.float32).astype(jnp.bfloat16)
        c_mid = part_sum.shape[3]
        interior = part_sum.reshape(num_images, groups, tile_rows, img_width, c_mid)
        zero_row = jnp.zeros((num_images, 1, img_width, c_mid), jnp.bfloat16)
        top_send = jnp.concatenate([zero_row, interior[:, :-1, tile_rows - 1]], axis=1)
        bottom_send = jnp.concatenate([interior[:, 1:, 0], zero_row], axis=1)
        edge_send = jnp.stack([top_send, bottom_send], axis=2)
        inner_recv = lax.all_to_all(interior, 'model', 1, 1, tiled=True)
        edge_recv = lax.all_to_all(edge_send, 'model', 1, 1, tiled=True)
        inner_sum = jnp.sum(inner_recv, axis=1, dtype=jnp.float32)
        edge_sum = jnp.sum(edge_recv, axis=1, dtype=jnp.float32)
        z_tile = jnp.concatenate([edge_sum[:, 0:1], inner_sum, edge_sum[:, 1:2]], axis=1)
        row_ids = my_index * tile_rows - 1 + jnp.arange(tile_rows + 2)
        inside = (row_ids >= 0) & (row_ids < height)
        hidden = jnp.where(inside[:, None, None], jax.nn.relu(z_tile + b_conv1), 0.0).astype(jnp.bfloat16)
        conv_two = lax.conv_general_dilated(hidden, w_conv2, (1, 1), ((0, 0), (1, 1)), dimension_numbers=CONV_LAYOUT, preferred_element_type=jnp.float32)
        c_out = conv_two.shape[3]
        short_part = jnp.einsum('bhwc,co->bhwo', images, w_short, preferred_element_type=jnp.float32).astype(jnp.bfloat16)
        short_part = short_part.reshape(num_images, groups, tile_rows, img_width, c_out)
        short_recv = lax.all_to_all(short_part, 'model', 1, 1, tiled=True)
        shortcut = jnp.sum(short_recv, axis=1, dtype=jnp.float32)
        return conv_two + b_conv2 + shortcut

    return jax.shard_map(local_step, mesh=mesh, in_specs=(P('data', None, None, 'model'), P(None, None, 'model', None), P(), P(), P(), P('model', None)), out_specs=P('data', 'model', None, None), check_vma=False)
```

profile of v0, /device:TPU:21, one launch (start us, length us, event | category | flops | bytes accessed | tf_op | source)
XLA Modules:
  0.0 2541.3 jit_solution(16421386973470499432)
XLA Ops:
  0.0 3.2 copy.68
  4.7 9.2 copy.44
  13.8 42.3 %select_convert_fusion = bf16[256,24,33,128]{3,1,2,0:T(8,128)(2,1)} fusion(pred[24,33]{0,1:T(8,128)(4,1)S(1)} %copy-done.7, bf16[256,24,35,4]{1,3,2,0:T(4,128)(2,1)} %copy.44, bf16[3,3,4,128]{3,2,1,0:T(4,128)(2,1)S(1)} %copy-done.5), kind=kOutput, calls=%fused_computation | convolution fusion | flops 1915600896 | bytes 53634840 | tf_op jit(solution)/shard_map/conv_general_dilated | solution.py:16
  56.1 34.8 %copy.45 = bf16[256,24,33,128]{3,0,2,1:T(8,128)(2,1)} copy(bf16[256,24,33,128]{3,1,2,0:T(8,128)(2,1)} %select_convert_fusion) | data formatting | bytes 103809024 | tf_op jit(solution)/shard_map/convert_element_type | solution.py:16
  90.9 33.7 %slice.21 = bf16[256,3,256,128]{3,0,2,1:T(8,128)(2,1)} slice(bf16[256,3,264,128]{3,0,2,1:T(8,128)(2,1)} %bitcast.43), slice={[0:256], [0:3], [0:256], [0:128]} | slice | bytes 100663296 | tf_op jit(solution)/shard_map/convert_element_type | solution.py:16
  124.6 19.7 fusion.15
  144.3 4.3 copy_bitcast_fusion.1
  152.4 3.1 copy.48
  155.5 11.3 all-to-all-start
  166.9 34.2 %copy.49 = bf16[3,16,16,256,128]{4,2,3,0,1:T(8,128)(2,1)} copy(bf16[3,16,16,256,128]{4,2,1,3,0:T(8,128)(2,1)} %bitcast.42) | data formatting | bytes 100663296 | tf_op jit(solution)/shard_map/reshape | solution.py:18
  201.1 106.7 %all-to-all-done = bf16[3,16,2,256,128]{4,3,0,2,1:T(8,128)(2,1)} async-done(((bf16[3,16,2,256,128]{4,3,0,2,1:T(8,128)(2,1)}), bf16[3,16,2,256,128]{4,3,0,2,1:T(8,128)(2,1)}, u32[]{:S(2)}, u32[]{:S(2)}) %all-to-all-start) | async-done | bytes 6291488 | tf_op jit(solution)/shard_map/all_to_all | solution.py:24
  307.8 9.0 all-to-all-start.1
  316.8 24.4 convolution_convert_fusion
  341.2 33.8 %copy.57 = bf16[3,16,16,256,128]{4,3,2,0,1:T(8,128)(2,1)} copy(bf16[3,16,16,256,128]{4,3,2,1,0:T(8,128)(2,1)} %bitcast.40) | data formatting | bytes 100663296 | tf_op jit(solution)/shard_map/reshape | solution.py:34
  375.0 1034.4 %all-to-all-done.1 = bf16[3,16,16,256,128]{4,2,3,0,1:T(8,128)(2,1)} async-done(((bf16[3,16,16,256,128]{4,2,3,0,1:T(8,128)(2,1)}), bf16[3,16,16,256,128]{4,2,3,0,1:T(8,128)(2,1)}, u32[]{:S(2)}, u32[]{:S(2)}) %all-to-all-start.1) | async-done | bytes 50331680 | tf_op jit(solution)/shard_map/all_to_all | solution.py:23
  1409.4 10.5 all-to-all-start.2
  1419.9 4.1 convert_reduce_fusion.2
  1424.0 19.1 convert_reduce_fusion.1
  1443.1 5.0 fusion.5
  1450.3 10.9 fusion.6
  1461.2 8.9 select_add_fusion
  1474.4 1038.0 %all-to-all-done.2 = bf16[3,16,16,256,128]{4,3,2,0,1:T(8,128)(2,1)} async-done(((bf16[3,16,16,256,128]{4,3,2,0,1:T(8,128)(2,1)}), bf16[3,16,16,256,128]{4,3,2,0,1:T(8,128)(2,1)}, u32[]{:S(2)}, u32[]{:S(2)}) %all-to-all-start.2) | async-done | bytes 50331680 | tf_op jit(solution)/shard_map/all_to_all | solution.py:35
  2512.4 19.1 convert_reduce_fusion
  2531.5 9.6 fusion.4
  (31 shorter events, 11.7 us)
Async XLA Ops:
  0.0 1461.2 %copy-start = (bf16[3,3,128,128]{3,2,1,0:T(8,128)(2,1)S(1)}, bf16[3,3,128,128]{3,2,1,0:T(8,128)(2,1)}, u32[]{:S(2)}) copy-start(bf16[3,3,128,128]{3,2,1,0:T(8,128)(2,1)} %param.9) | copy-start | bytes 884740
  4.6 9.2 copy-start.5
  4.7 9.2 copy-start.7
  148.7 2.7 copy-start.1
  155.5 152.2 %all-to-all-start = ((bf16[3,16,2,256,128]{4,3,0,2,1:T(8,128)(2,1)}), bf16[3,16,2,256,128]{4,3,0,2,1:T(8,128)(2,1)}, u32[]{:S(2)}, u32[]{:S(2)}) async-start(bf16[3,16,2,256,128]{4,3,0,2,1:T(8,128)(2,1)} %copy.48), calls=%async_computation | async-start | bytes 12582912 | tf_op jit(solution)/shard_map/all_to_all | solution.py:24
  201.1 115.7 %copy-start.2 = (bf16[3,256,256,4]{2,3,1,0:T(4,128)(2,1)S(1)}, bf16[3,256,256,4]{2,3,1,0:T(4,128)(2,1)}, u32[]{:S(2)}) copy-start(bf16[3,256,256,4]{2,3,1,0:T(4,128)(2,1)} %param.6) | copy-start | bytes 4718596
  201.1 115.7 %copy-start.3 = (bf16[4,128]{1,0:T(4,128)(2,1)S(1)}, bf16[4,128]{1,0:T(4,128)(2,1)}, u32[]{:S(2)}) copy-start(bf16[4,128]{1,0:T(4,128)(2,1)} %param.11) | copy-start | bytes 3076
  307.8 1101.6 %all-to-all-start.1 = ((bf16[3,16,16,256,128]{4,2,3,0,1:T(8,128)(2,1)}), bf16[3,16,16,256,128]{4,2,3,0,1:T(8,128)(2,1)}, u32[]{:S(2)}, u32[]{:S(2)}) async-start(bf16[3,16,16,256,128]{4,2,3,0,1:T(8,128)(2,1)} %copy.49), calls=%async_computation.1 | async-start | bytes 100663296 | tf_op jit(solution)/shard_map/all_to_all | solution.py:23
  1409.4 1103.1 %all-to-all-start.2 = ((bf16[3,16,16,256,128]{4,3,2,0,1:T(8,128)(2,1)}), bf16[3,16,16,256,128]{4,3,2,0,1:T(8,128)(2,1)}, u32[]{:S(2)}, u32[]{:S(2)}) async-start(bf16[3,16,16,256,128]{4,3,2,0,1:T(8,128)(2,1)} %copy.57), calls=%async_computation.2 | async-start | bytes 100663296 | tf_op jit(solution)/shard_map/all_to_all | solution.py:35
  1424.0 19.1 copy-start.4
  1450.1 11.1 copy-start.6
  1450.1 11.1 copy-start.8
where the time goes:
time: 2550 us; the launch traced here: 2540 us
  waiting for transfers between devices  2180 us (85%)
  local copies, waits for them, and re-layouts  186 us (7%)
  matrix products  75.5 us (3%)
  other arithmetic  69 us (3%)
  starting transfers between devices  30.9 us (1%)
    all_to_all x1, waiting for transfers between devices, local_step(): short_recv = lax.all_to_all(short_part, 'model', 1, 1, tiled=True)  1040 us
    all_to_all x1, waiting for transfers between devices, local_step(): inner_recv = lax.all_to_all(interior, 'model', 1, 1, tiled=True)  1030 us
    all_to_all x1, waiting for transfers between devices, local_step(): edge_recv = lax.all_to_all(edge_send, 'model', 1, 1, tiled=True)  107 us
    convert_element_type x2, local copies, waits for them, and re-layouts, local_step(): lax.conv_general_dilated(images, w_conv1, (1, 1), 'SAME', dimension_numbe...  68.5 us
  transfers between devices with their start and end apart: 3, of which 3 were waited for; matrix products, arithmetic and copies ran while one was open for 6% of the time, Pallas kernels for 0%

commit v1 on v0

v1 whole, which is shorter than its diff:
```python
import functools

import jax
import jax.numpy as jnp
from jax import lax
from jax.experimental import pallas as pl
from jax.experimental.pallas import tpu as pltpu
from jax.sharding import PartitionSpec as P

MESH = pl.DeviceIdType.MESH
LANES = 128


def shift_right(v):
    return jnp.concatenate([jnp.zeros((v.shape[0], 1), v.dtype), v[:, :-1]], axis=1)


def shift_left(v):
    return jnp.concatenate([v[:, 1:], jnp.zeros((v.shape[0], 1), v.dtype)], axis=1)


def kernel(n, x_ref, w1_ref, b1_ref, w2_ref, b2_ref, ws_ref, out_ref,
           xbuf, gw, gs, wk, wt, sk, st, w2t, y1s, sbuf, ybuf,
           send_x, recv_x, send_h, recv_top, recv_bot, send_w, recv_w, send_v, recv_v, out_sem):
    ni, height, ch, width = x_ref.shape
    halves = width // LANES
    tile = height // n
    nz = n // 2
    c_mid = w1_ref.shape[3]
    c_out = ws_ref.shape[1]
    me = lax.axis_index('model')
    my_z, my_c = me // 2, me % 2
    sibling = me + 1 - 2 * my_c

    barrier = pltpu.get_barrier_semaphore()
    for k in range(1, n):
        pl.semaphore_signal(barrier, inc=1, device_id={'model': (me + k) % n}, device_id_type=MESH)

    def own_rows(img, h):
        return pltpu.make_async_copy(
            x_ref.at[img, pl.ds(me * tile, tile), :, pl.ds(h * LANES, LANES)],
            xbuf.at[img, me, h, pl.ds(2, tile)], recv_x.at[img])

    for img in range(ni):
        for h in range(halves):
            own_rows(img, h).start()
    own_w = pltpu.make_async_copy(w1_ref, gw.at[my_z, my_c], recv_w.at[0])
    own_s = pltpu.make_async_copy(ws_ref, gs.at[my_z, my_c], recv_w.at[1])
    own_w.start()
    own_s.start()

    pl.semaphore_wait(barrier, n - 1)

    def send_rows(img, dest, h):
        return pltpu.make_async_remote_copy(
            src_ref=x_ref.at[img, pl.ds(dest * tile, tile), :, pl.ds(h * LANES, LANES)],
            dst_ref=xbuf.at[img, me, h, pl.ds(2, tile)],
            send_sem=send_x, recv_sem=recv_x.at[img], device_id={'model': dest}, device_id_type=MESH)

    hops = [nz // 2]
    for d in range(nz // 2 - 1, 0, -1):
        hops += [d, nz - d]

    def send_image(img):
        for d in hops:
            for c in range(2):
                dest = ((my_z + d) % nz) * 2 + (my_c + c) % 2
                for h in range(halves):
                    send_rows(img, dest, h).start()
        for h in range(halves):
            send_rows(img, sibling, h).start()

    send_image(0)
    for d in hops:
        dest = ((my_z + d) % nz) * 2 + my_c
        pltpu.make_async_remote_copy(
            src_ref=w1_ref, dst_ref=gw.at[my_z, my_c], send_sem=send_w.at[0], recv_sem=recv_w.at[0],
            device_id={'model': dest}, device_id_type=MESH).start()
        pltpu.make_async_remote_copy(
            src_ref=ws_ref, dst_ref=gs.at[my_z, my_c], send_sem=send_w.at[1], recv_sem=recv_w.at[1],
            device_id={'model': dest}, device_id_type=MESH).start()
    for img in range(1, ni):
        send_image(img)

    @pl.when(me == 0)
    def _():
        for img in range(ni):
            for h in range(halves):
                xbuf[img, :, h, 0:2] = jnp.zeros((n, 2, ch, LANES), xbuf.dtype)

    @pl.when(me == n - 1)
    def _():
        for img in range(ni):
            for h in range(halves):
                xbuf[img, :, h, tile + 2:tile + 4] = jnp.zeros((n, 2, ch, LANES), xbuf.dtype)

    for t in range(9):
        w2t[:, t * c_mid:(t + 1) * c_mid] = w2_ref[t // 3, t % 3].astype(jnp.float32).T.astype(w2t.dtype)
    wk[...] = jnp.zeros_like(wk)
    sk[...] = jnp.zeros_like(sk)

    for k, ref in enumerate((gw.at[:, my_c], gs.at[:, my_c])):
        pltpu.make_async_remote_copy(src_ref=ref, dst_ref=ref, send_sem=send_v.at[k], recv_sem=recv_w.at[k],
                                     device_id={'model': sibling}, device_id_type=MESH).wait_recv()

    share_w = pltpu.make_async_remote_copy(
        src_ref=gw.at[:, my_c], dst_ref=gw.at[:, my_c], send_sem=send_v.at[0], recv_sem=recv_v.at[0],
        device_id={'model': sibling}, device_id_type=MESH)
    share_s = pltpu.make_async_remote_copy(
        src_ref=gs.at[:, my_c], dst_ref=gs.at[:, my_c], send_sem=send_v.at[1], recv_sem=recv_v.at[1],
        device_id={'model': sibling}, device_id_type=MESH)
    share_w.start()
    share_s.start()
    share_w.wait()
    share_s.wait()

    def place(z, _):
        for c in range(2):
            src = z * 2 + c
            for dh in range(3):
                for dw in range(3):
                    piece = gw[z, c, dh, dw].astype(jnp.float32)
                    for a in range(2):
                        wk[dw, src, (dh + a) * ch:(dh + a + 1) * ch, a * c_mid:(a + 1) * c_mid] = piece
            piece = gs[z, c].astype(jnp.float32)
            for a in range(2):
                sk[src, (1 + a) * ch:(2 + a) * ch, a * c_out:(a + 1) * c_out] = piece
        return 0

    lax.fori_loop(0, nz, place, 0)
    kb = n * 4 * ch
    for dw in range(3):
        wt[:, dw * kb:(dw + 1) * kb] = wk[dw].reshape(kb, 2 * c_mid).T.astype(wt.dtype)
    st[...] = sk[...].reshape(kb, 2 * c_out).T.astype(st.dtype)

    xk = xbuf.reshape(ni, n, halves, (tile + 4) * ch, LANES)
    b1_col = b1_ref[...]
    b2_row = b2_ref[...]

    def pair(img, p):
        x0 = jnp.concatenate(
            [xk[img, :, h, pl.ds(pl.multiple_of(p * 2 * ch, 2 * ch), 4 * ch), :].reshape(kb, LANES) for h in range(halves)], axis=1)
        rhs = jnp.concatenate([shift_right(x0), x0, shift_left(x0)], axis=0)
        z2 = jnp.dot(wt[...], rhs, preferred_element_type=jnp.float32)
        s2 = jnp.dot(st[...], x0, preferred_element_type=jnp.float32)
        for a in range(2):
            y = jnp.maximum(z2[a * c_mid:(a + 1) * c_mid] + b1_col, 0.0)
            row = me * tile - 1 + 2 * p + a
            y = jnp.where((row >= 0) & (row < height), y, 0.0).astype(jnp.bfloat16)
            base = pl.multiple_of((2 * p + a) * 3 * c_mid, 3 * c_mid)
            y1s[pl.ds(base, c_mid), :] = shift_right(y)
            y1s[pl.ds(base + c_mid, c_mid), :] = y
            y1s[pl.ds(base + 2 * c_mid, c_mid), :] = shift_left(y)
            sbuf[2 * p + a] = s2[a * c_out:(a + 1) * c_out]

    def out_copy(img, r):
        return pltpu.make_async_copy(ybuf.at[img, r], out_ref.at[img, r], out_sem)

    def second(img, r):
        rhs = y1s[pl.ds(pl.multiple_of(r * 3 * c_mid, 3 * c_mid), 9 * c_mid), :]
        y2 = jnp.dot(w2t[...], rhs, preferred_element_type=jnp.float32) + sbuf[r + 1]
        ybuf[img, r] = y2.T + b2_row
        out_copy(img, r).start()

    def halo(img, src_row, dst_row, dest, k, recv):
        return pltpu.make_async_remote_copy(
            src_ref=xbuf.at[img, :, :, pl.ds(src_row, 2)], dst_ref=xbuf.at[img, :, :, pl.ds(dst_row, 2)],
            send_sem=send_h.at[img, k], recv_sem=recv.at[img], device_id={'model': dest}, device_id_type=MESH)

    def up(img):
        return halo(img, 2, tile + 2, me - 1, 0, recv_bot)

    def down(img):
        return halo(img, tile, 0, me + 1, 1, recv_top)

    def one_image(img, _):
        pltpu.make_async_remote_copy(
            src_ref=xbuf.at[img, :, :, pl.ds(2, tile)], dst_ref=xbuf.at[img, :, :, pl.ds(2, tile)],
            send_sem=send_x, recv_sem=recv_x.at[img], device_id={'model': sibling}, device_id_type=MESH).wait_recv()

        @pl.when(me > 0)
        def _():
            up(img).start()

        @pl.when(me < n - 1)
        def _():
            down(img).start()

        def inner(p, _):
            pair(img, p)
            return 0

        lax.fori_loop(1, tile // 2, inner, 0)

        @pl.when(me > 0)
        def _():
            halo(img, 2, 0, me, 1, recv_top).wait_recv()

        @pl.when(me < n - 1)
        def _():
            halo(img, 2, tile + 2, me, 0, recv_bot).wait_recv()

        def edge(q, _):
            pair(img, q * (tile // 2))
            return 0

        lax.fori_loop(0, 2, edge, 0)

        def rows(r, _):
            second(img, r)
            return 0

        lax.fori_loop(0, tile, rows, 0, unroll=2)
        return 0

    lax.fori_loop(0, ni, one_image, 0)

    pltpu.make_async_copy(ybuf, out_ref, out_sem).wait()
    sent = xbuf.at[:, pl.ds(0, n - 1), :, pl.ds(2, tile)]
    pltpu.make_async_remote_copy(src_ref=sent, dst_ref=sent, send_sem=send_x, recv_sem=recv_x.at[0],
                                 device_id={'model': sibling}, device_id_type=MESH).wait_send()
    sent_w, sent_s = gw.at[pl.ds(0, nz - 1), 0], gs.at[pl.ds(0, nz - 1), 0]
    for k, ref in enumerate((sent_w, sent_s)):
        pltpu.make_async_remote_copy(src_ref=ref, dst_ref=ref, send_sem=send_w.at[k], recv_sem=recv_w.at[k],
                                     device_id={'model': sibling}, device_id_type=MESH).wait_send()
    for img in range(ni):
        @pl.when(me > 0)
        def _():
            up(img).wait_send()

        @pl.when(me < n - 1)
        def _():
            down(img).wait_send()


def solution(mesh):
    n = mesh.shape['model']

    def local_step(images, w_conv1, b_conv1, w_conv2, b_conv2, w_short):
        x = images.transpose(0, 1, 3, 2)
        ni, height, ch, width = x.shape
        c_mid, c_out = w_conv1.shape[3], w_short.shape[1]
        tile, halves, nz = height // n, width // LANES, n // 2
        kb = n * 4 * ch
        vmem = pl.BlockSpec(memory_space=pltpu.VMEM)
        hbm = pl.BlockSpec(memory_space=pl.ANY)
        dma = pltpu.SemaphoreType.DMA
        return pl.pallas_call(
            functools.partial(kernel, n),
            out_shape=jax.ShapeDtypeStruct((ni, tile, width, c_out), jnp.float32),
            in_specs=[hbm, hbm, vmem, vmem, vmem, hbm],
            out_specs=hbm,
            scratch_shapes=[
                pltpu.VMEM((ni, n, halves, tile + 4, ch, LANES), jnp.bfloat16),
                pltpu.VMEM((nz, 2, 3, 3, ch, c_mid), jnp.bfloat16),
                pltpu.VMEM((nz, 2, ch, c_out), jnp.bfloat16),
                pltpu.VMEM((3, n, 4 * ch, 2 * c_mid), jnp.float32),
                pltpu.VMEM((2 * c_mid, 3 * kb), jnp.bfloat16),
                pltpu.VMEM((n, 4 * ch, 2 * c_out), jnp.float32),
                pltpu.VMEM((2 * c_out, kb), jnp.bfloat16),
                pltpu.VMEM((c_out, 9 * c_mid), jnp.bfloat16),
                pltpu.VMEM(((tile + 2) * 3 * c_mid, width), jnp.bfloat16),
                pltpu.VMEM((tile + 2, c_out, width), jnp.float32),
                pltpu.VMEM((ni, tile, width, c_out), jnp.float32),
                dma, dma((ni,)), dma((ni, 2)), dma((ni,)), dma((ni,)), dma((2,)), dma((2,)), dma((2,)), dma((2,)), dma,
            ],
            compiler_params=pltpu.CompilerParams(collective_id=0, has_side_effects=True),
        )(x, w_conv1, b_conv1.reshape(c_mid, 1), w_conv2, b_conv2.reshape(1, c_out), w_short)

    return jax.shard_map(local_step, mesh=mesh, in_specs=(P('data', None, None, 'model'), P(None, None, 'model', None), P(), P(), P(), P('model', None)), out_specs=P('data', 'model', None, None), check_vma=False)
```

time: 2550 us -> 77.3 us (0.03)
  waiting for transfers between devices: 2180 us -> 0 us
  local copies, waits for them, and re-layouts: 186 us -> 7.58 us
  matrix products: 75.5 us -> 0 us
  Pallas kernels: 0 us -> 69.6 us
  other arithmetic: 69 us -> 0 us
  starting transfers between devices: 30.9 us -> 0 us
    all_to_all x3 -> x0, waiting for transfers between devices: 2180 us -> none  [the longest x1 1040 us: local_step(): short_recv = lax.all_to_all(short_part, 'model', 1, 1, tiled=True)]
    pallas_call x0 -> x1, Pallas kernels: none -> 69.6 us  [local_step(): pl.pallas_call(functools.partial(kernel, n), out_shape=jax.ShapeDtypeStru...]
    convert_element_type x3 -> x0, local copies, waits for them, and re-layouts: 69.4 us -> none  [the longest x2 68.5 us: local_step(): lax.conv_general_dilated(images, w_conv1, (1, 1), 'SAME', dimension_numbe...]
    reshape x2 -> x1, local copies, waits for them, and re-layouts: 68 us -> 1.39 us  [local_step(): b_conv1.reshape(c_mid, 1)]
    conv_general_dilated x2 -> x0, matrix products: 51.1 us -> none  [the longest x1 42.3 us: local_step(): lax.conv_general_dilated(images, w_conv1, (1, 1), 'SAME', dimension_numbe...]
    reduce_sum x3 -> x0, other arithmetic: 42.2 us -> none  [the longest x1 19.1 us: local_step(): shortcut = jnp.sum(short_recv, axis=1, dtype=jnp.float32)]
    all_to_all x3 -> x0, starting transfers between devices: 30.9 us -> none  [the longest x1 11.3 us: local_step(): edge_recv = lax.all_to_all(edge_send, 'model', 1, 1, tiled=True)]
  transfers between devices with their start and end apart: 3 -> 0, of which waited for: 3 -> 0; matrix products, arithmetic and copies ran while one was open for 6% -> 0% of each run, Pallas kernels for 0% -> 0%
where the time goes in v1:
time: 77.3 us; the launch traced here: 77.2 us
  Pallas kernels  69.6 us (90%)
  local copies, waits for them, and re-layouts  7.58 us (10%)
    pallas_call x1, Pallas kernels, local_step(): pl.pallas_call(functools.partial(kernel, n), out_shape=jax.ShapeDtypeStru...  69.6 us
    unnamed x1, local copies, waits for them, and re-layouts  6.2 us

profile of v1, /device:TPU:21, one launch (start us, length us, event | category | flops | bytes accessed | tf_op | source)
XLA Modules:
  0.0 77.2 jit_solution(73600630575497787)
XLA Ops:
  0.0 1.4 %copy.7.b1_ref = f32[128,1]{1,0:T(8,128)} copy(f32[128,1]{0,1:T(1,128)} %bitcast.4) | data formatting | bytes 1024 | tf_op jit(solution)/shard_map/reshape | solution.py:268
  1.4 69.6 %shard_map.64 = f32[3,16,256,128]{3,2,1,0:T(8,128)} custom-call(bf16[3,256,4,256]{3,2,1,0:T(4,128)(2,1)} %bitcast.3, bf16[3,3,4,128]{3,2,1,0:T(4,128)(2,1)} %w1_ref.1, f32[128,1]{1,0:T(8,128)} %copy.7.b1_ref, bf16[3,3,128,128]{3,2,1,0:T(8,128)(2,1)} %w2_ref.1, f32[1,128]{1,0:T(1,128)} %bitcast.5, bf16[4,128]{1,0:T(4,128)(2,1)} %ws_ref.1), custom_call_target="tpu_custom_call" | custom-call | tf_op jit(solution)/shard_map/pallas_call | solution.py:248
  71.0 6.2 %copy.9 = f32[3,16,256,128]{3,2,1,0:T(8,128)} copy(f32[3,16,256,128]{3,2,1,0:T(8,128)} %shard_map.64) | data formatting | bytes 12582912

commit v2 on v0

v2 whole, which is shorter than its diff:
```python
import functools

import jax
import jax.numpy as jnp
from jax import lax
from jax.experimental import pallas as pl
from jax.experimental.pallas import tpu as pltpu
from jax.sharding import PartitionSpec as P

MESH = pl.DeviceIdType.MESH
LANES = 128
EDGE = 4


def shift_right(v):
    return jnp.concatenate([jnp.zeros((v.shape[0], 1), v.dtype), v[:, :-1]], axis=1)


def shift_left(v):
    return jnp.concatenate([v[:, 1:], jnp.zeros((v.shape[0], 1), v.dtype)], axis=1)


def first_pair(n, height, img, p, xbuf, wt, st, b1c, y1s, sbuf):
    ni, _, halves, rows, ch, _ = xbuf.shape
    tile = rows - 4
    c_mid, c_out = wt.shape[0] // 2, st.shape[0] // 2
    kb = n * 4 * ch
    me = lax.axis_index('model')
    xk = xbuf.reshape(ni, n, halves, rows * ch, LANES)
    start = p * (2 * ch) if isinstance(p, int) else pl.multiple_of(p * 2 * ch, 2 * ch)
    x0 = jnp.concatenate([xk[img, :, h, pl.ds(start, 4 * ch), :].reshape(kb, LANES) for h in range(halves)], axis=1)
    rhs = jnp.concatenate([shift_right(x0), x0, shift_left(x0)], axis=0)
    z2 = jnp.dot(wt[...], rhs, preferred_element_type=jnp.float32)
    s2 = jnp.dot(st[...], x0, preferred_element_type=jnp.float32)
    for a in range(2):
        y = jnp.maximum(z2[a * c_mid:(a + 1) * c_mid] + b1c[:, 0:1], 0.0)
        row = me * tile - 1 + 2 * p + a
        y = jnp.where((row >= 0) & (row < height), y, 0.0).astype(jnp.bfloat16)
        base = (2 * p + a) * 3 * c_mid
        if not isinstance(p, int):
            base = pl.multiple_of(base, c_mid)
        y1s[pl.ds(base, c_mid), :] = shift_right(y)
        y1s[pl.ds(base + c_mid, c_mid), :] = y
        y1s[pl.ds(base + 2 * c_mid, c_mid), :] = shift_left(y)
        sbuf[2 * p + a] = s2[a * c_out:(a + 1) * c_out]


def second_row(r, w2t, b2_ref, y1s, sbuf):
    c_mid = w2t.shape[1] // 9
    base = r * 3 * c_mid
    if not isinstance(r, int):
        base = pl.multiple_of(base, c_mid)
    y2 = jnp.dot(w2t[...], y1s[pl.ds(base, 9 * c_mid), :], preferred_element_type=jnp.float32) + sbuf[r + 1]
    return y2.T + b2_ref[...]


def loop(lo, hi, body, unroll=1):
    def step(i, _):
        body(i)
        return 0

    lax.fori_loop(lo, hi, step, 0, unroll=unroll)


def gather_kernel(n, x_ref, w1_ref, b1_hbm, w2_hbm, b2_hbm, ws_ref,
                  xbuf, wt, st, w2t, b1c, b2_ref, y1s, sbuf, y2,
                  gw, gs, wk, sk, w2_ref, b1_ref,
                  local, phase, send_x, recv_x, send_h, recv_top, recv_bot, send_w, recv_w, send_v, recv_v):
    ni, height, ch, width = x_ref.shape
    halves = width // LANES
    tile = height // n
    nz = n // 2
    last = ni - 1
    c_mid, c_out = w1_ref.shape[3], ws_ref.shape[1]
    kb = n * 4 * ch
    me = lax.axis_index('model')
    my_z, my_c = me // 2, me % 2
    sibling = me + 1 - 2 * my_c

    def core(d, c):
        return ((my_z + d) % nz) * 2 + (my_c + c) % 2

    barrier = pltpu.get_barrier_semaphore()
    for dest in (sibling, core(1, 0), core(1, 1), core(nz - 1, 0), core(nz - 1, 1)):
        pl.semaphore_signal(barrier, inc=1, device_id={'model': dest}, device_id_type=MESH)

    whole = [((0, tile), img) for img in range(last)]
    ends = [((0, EDGE), last), ((tile - EDGE, EDGE), last)]
    middle = [((EDGE, tile - 2 * EDGE), ni)]

    def ends_of(img, part, h, dest):
        (r0, rows), k = part
        return (x_ref.at[img, pl.ds(dest * tile + r0, rows), :, pl.ds(h * LANES, LANES)],
                xbuf.at[img, me, h, pl.ds(2 + r0, rows)], recv_x.at[k])

    def keep(img, parts):
        for part in parts:
            for h in range(halves):
                src, dst, sem = ends_of(img, part, h, me)
                pltpu.make_async_copy(src, dst, sem).start()

    def send(img, parts, hops):
        for d in hops:
            for c in range(2) if d else (1,):
                dest = core(d, c)
                for part in parts:
                    for h in range(halves):
                        src, dst, sem = ends_of(img, part, h, dest)
                        pltpu.make_async_remote_copy(src_ref=src, dst_ref=dst, send_sem=send_x, recv_sem=sem,
                                                     device_id={'model': dest}, device_id_type=MESH).start()

    def send_weights(hops):
        for d in hops:
            for k, (src, dst) in enumerate(((w1_ref, gw), (ws_ref, gs))):
                pltpu.make_async_remote_copy(
                    src_ref=src, dst_ref=dst.at[my_z, my_c], send_sem=send_w.at[k], recv_sem=recv_w.at[k],
                    device_id={'model': core(d, 0)}, device_id_type=MESH).start()

    def arrived(ref, sem):
        pltpu.make_async_remote_copy(src_ref=ref, dst_ref=ref, send_sem=send_x, recv_sem=sem,
                                     device_id={'model': sibling}, device_id_type=MESH).wait_recv()

    for img in range(last):
        keep(img, [whole[img]])
    keep(last, ends + middle)
    pltpu.make_async_copy(w1_ref, gw.at[my_z, my_c], recv_w.at[0]).start()
    pltpu.make_async_copy(ws_ref, gs.at[my_z, my_c], recv_w.at[1]).start()

    fetches = [pltpu.make_async_copy(src, dst, local.at[k])
               for k, (src, dst) in enumerate(((b1_hbm, b1_ref), (b2_hbm, b2_ref), (w2_hbm, w2_ref)))]
    for fetch in fetches:
        fetch.start()

    pl.semaphore_wait(barrier, 5)
    for d in range(1, nz // 2 + 1):
        if d < nz // 2:
            for side in (1, nz - 1):
                pl.semaphore_signal(phase.at[d - 1], inc=1, device_id={'model': core(side, 0)}, device_id_type=MESH)
        send(0, [whole[0]], [d, nz - d] if d < nz // 2 else [d])
        if d < nz // 2:
            pl.semaphore_wait(phase.at[d - 1], 2)
    send(0, [whole[0]], [0])
    near = [d for k in range(1, nz // 2) for d in (k, nz - k)]
    far = [nz // 2] + near[::-1]
    first, rest = far[:3], far[3:] + [0]
    send_weights(far)
    send(1, [whole[1]], first)

    for owner, r0 in ((0, 0), (n - 1, tile + 2)):
        @pl.when(me == owner)
        def _():
            for img in range(ni):
                for h in range(halves):
                    xbuf[img, :, h, r0:r0 + 2] = jnp.zeros((n, 2, ch, LANES), xbuf.dtype)

    for fetch in fetches:
        fetch.wait()
    b1c[...] = jnp.broadcast_to(b1_ref[...], (c_mid, c_mid)).T
    for t in range(9):
        w2t[:, t * c_mid:(t + 1) * c_mid] = w2_ref[t // 3, t % 3].astype(jnp.float32).T.astype(w2t.dtype)
    wk[...] = jnp.zeros_like(wk)
    sk[...] = jnp.zeros_like(sk)

    shares = []
    for k, ref in enumerate((gw.at[:, my_c], gs.at[:, my_c])):
        arrived(ref, recv_w.at[k])
        shares.append(pltpu.make_async_remote_copy(
            src_ref=ref, dst_ref=ref, send_sem=send_v.at[k], recv_sem=recv_v.at[k],
            device_id={'model': sibling}, device_id_type=MESH))
        shares[k].start()
    for share in shares:
        share.wait()

    def place(z):
        for c in range(2):
            src = z * 2 + c
            for dh in range(3):
                for dw in range(3):
                    piece = gw[z, c, dh, dw].astype(jnp.float32)
                    for a in range(2):
                        wk[dw, src, (dh + a) * ch:(dh + a + 1) * ch, a * c_mid:(a + 1) * c_mid] = piece
            piece = gs[z, c].astype(jnp.float32)
            for a in range(2):
                sk[src, (1 + a) * ch:(2 + a) * ch, a * c_out:(a + 1) * c_out] = piece

    loop(0, nz, place)
    for dw in range(3):
        wt[:, dw * kb:(dw + 1) * kb] = wk[dw].reshape(kb, 2 * c_mid).T.astype(wt.dtype)
    st[...] = sk[...].reshape(kb, 2 * c_out).T.astype(st.dtype)

    def pair(img, p):
        first_pair(n, height, img, p, xbuf, wt, st, b1c, y1s, sbuf)

    def second(img, r):
        y2[img, r] = second_row(r, w2t, b2_ref, y1s, sbuf)

    def halo(img, src_row, dst_row, dest, k, recv):
        return pltpu.make_async_remote_copy(
            src_ref=xbuf.at[img, :, :, pl.ds(src_row, 2)], dst_ref=xbuf.at[img, :, :, pl.ds(dst_row, 2)],
            send_sem=send_h.at[img, k], recv_sem=recv.at[img], device_id={'model': dest}, device_id_type=MESH)

    def halo_up(img):
        return halo(img, 2, tile + 2, me - 1, 0, recv_bot)

    def halo_down(img):
        return halo(img, tile, 0, me + 1, 1, recv_top)

    def start_halos(img):
        @pl.when(me > 0)
        def _():
            halo_up(img).start()

        @pl.when(me < n - 1)
        def _():
            halo_down(img).start()

    def wait_halos(img):
        @pl.when(me > 0)
        def _():
            halo(img, 2, 0, me, 1, recv_top).wait_recv()

        @pl.when(me < n - 1)
        def _():
            halo(img, 2, tile + 2, me, 0, recv_bot).wait_recv()

    last_pair = tile // 2
    for img in range(last):
        arrived(xbuf.at[img, :, :, pl.ds(2, tile)], recv_x.at[img])
        start_halos(img)
        if img + 1 < last:
            send(img + 1, [whole[img + 1]], rest)
        else:
            send(last, middle, far + [0])
        loop(1, last_pair, lambda p: pair(img, p))
        loop(2, tile - 2, lambda r: second(img, r), unroll=2)
        if img + 2 < last:
            send(img + 2, [whole[img + 2]], first)
        elif img + 2 == last:
            send(last, ends, far + [0])
        wait_halos(img)
        loop(0, 2, lambda q: pair(img, q * last_pair))
        loop(0, 2, lambda q: [second(img, q * (tile - 2) + k) for k in range(2)])

    arrived(xbuf.at[last, :, :, pl.ds(2, 2 * EDGE)], recv_x.at[last])
    start_halos(last)
    wait_halos(last)
    loop(0, 4, lambda q: pair(last, q + (q // 2) * (last_pair - 3)))
    loop(0, 2, lambda q: [second(last, q * (tile - 2) + k) for k in range(2)])

    sent = xbuf.at[:, pl.ds(0, n - 1), :, pl.ds(2, tile)]
    pltpu.make_async_remote_copy(src_ref=sent, dst_ref=sent, send_sem=send_x, recv_sem=recv_x.at[0],
                                 device_id={'model': sibling}, device_id_type=MESH).wait_send()
    for k, ref in enumerate((gw.at[pl.ds(0, nz - 1), 0], gs.at[pl.ds(0, nz - 1), 0])):
        pltpu.make_async_remote_copy(src_ref=ref, dst_ref=ref, send_sem=send_w.at[k], recv_sem=recv_w.at[k],
                                     device_id={'model': sibling}, device_id_type=MESH).wait_send()
    for img in range(ni):
        @pl.when(me > 0)
        def _():
            halo_up(img).wait_send()

        @pl.when(me < n - 1)
        def _():
            halo_down(img).wait_send()
    arrived(xbuf.at[last, :, :, pl.ds(2 + EDGE, tile - 2 * EDGE)], recv_x.at[ni])


def finish_kernel(n, height, xbuf, wt, st, w2t, b1c, b2_ref, y1s_in, sbuf_in, y2, out_ref, y1s, sbuf, yb, sem):
    ni, tile = y2.shape[0], y2.shape[1]
    last = ni - 1
    copies = [pltpu.make_async_copy(y2.at[pl.ds(0, last)], out_ref.at[pl.ds(0, last)], sem.at[0])]
    for k, r in enumerate((0, tile - 2)):
        copies.append(pltpu.make_async_copy(y2.at[last, pl.ds(r, 2)], out_ref.at[last, pl.ds(r, 2)], sem.at[1 + k]))
    for copy in copies:
        copy.start()
    step = 3 * b1c.shape[0]
    for i in (2, tile - 2):
        y1s[i * step:(i + 2) * step] = y1s_in[i * step:(i + 2) * step]
    for i in (3, tile - 2):
        sbuf[i] = sbuf_in[i]
    loop(EDGE // 2, tile // 2 + 1 - EDGE // 2, lambda p: first_pair(n, height, last, p, xbuf, wt, st, b1c, y1s, sbuf))

    def row(r):
        yb[r - 2] = second_row(r, w2t, b2_ref, y1s, sbuf)
        pltpu.make_async_copy(yb.at[r - 2], out_ref.at[last, r], sem.at[3]).start()

    loop(2, tile - 2, row, unroll=2)
    for copy in copies:
        copy.wait()
    pltpu.make_async_copy(yb, out_ref.at[last, pl.ds(2, tile - 4)], sem.at[3]).wait()


def solution(mesh):
    n = mesh.shape['model']

    def local_step(images, w_conv1, b_conv1, w_conv2, b_conv2, w_short):
        x = images.transpose(0, 1, 3, 2)
        ni, height, ch, width = x.shape
        c_mid, c_out = w_conv1.shape[3], w_short.shape[1]
        tile, halves, nz = height // n, width // LANES, n // 2
        kb = n * 4 * ch
        vmem = pl.BlockSpec(memory_space=pltpu.VMEM)
        hbm = pl.BlockSpec(memory_space=pltpu.HBM)
        dma = pltpu.SemaphoreType.DMA
        y1s = pltpu.VMEM(((tile + 2) * 3 * c_mid, width), jnp.bfloat16)
        sbuf = pltpu.VMEM((tile + 2, c_out, width), jnp.float32)
        parts = pl.pallas_call(
            functools.partial(gather_kernel, n),
            out_shape=[
                pltpu.VMEM((ni, n, halves, tile + 4, ch, LANES), jnp.bfloat16),
                pltpu.VMEM((2 * c_mid, 3 * kb), jnp.bfloat16),
                pltpu.VMEM((2 * c_out, kb), jnp.bfloat16),
                pltpu.VMEM((c_out, 9 * c_mid), jnp.bfloat16),
                pltpu.VMEM((c_mid, c_mid), jnp.float32),
                pltpu.VMEM((1, c_out), jnp.float32),
                y1s,
                sbuf,
                pltpu.VMEM((ni, tile, width, c_out), jnp.float32),
            ],
            in_specs=[hbm] * 6,
            out_specs=[vmem] * 9,
            scratch_shapes=[
                pltpu.VMEM((nz, 2, 3, 3, ch, c_mid), jnp.bfloat16),
                pltpu.VMEM((nz, 2, ch, c_out), jnp.bfloat16),
                pltpu.VMEM((3, n, 4 * ch, 2 * c_mid), jnp.float32),
                pltpu.VMEM((n, 4 * ch, 2 * c_out), jnp.float32),
                pltpu.VMEM(w_conv2.shape, w_conv2.dtype),
                pltpu.VMEM((1, c_mid), jnp.float32),
                dma((3,)), pltpu.SemaphoreType.REGULAR((nz // 2,)),
                dma, dma((ni + 1,)), dma((ni, 2)), dma((ni,)), dma((ni,)), dma((2,)), dma((2,)), dma((2,)), dma((2,)),
            ],
            compiler_params=pltpu.CompilerParams(collective_id=0, has_side_effects=True, vmem_limit_bytes=20 * 2**20),
        )(*[pltpu.with_memory_space_constraint(v, pltpu.HBM) for v in (x, w_conv1, b_conv1.reshape(1, c_mid), w_conv2, b_conv2.reshape(1, c_out), w_short)])
        return pl.pallas_call(
            functools.partial(finish_kernel, n, height),
            out_shape=jax.ShapeDtypeStruct((ni, tile, width, c_out), jnp.float32),
            in_specs=[vmem] * 9,
            out_specs=hbm,
            scratch_shapes=[y1s, sbuf, pltpu.VMEM((tile - 4, width, c_out), jnp.float32), dma((4,))],
            compiler_params=pltpu.CompilerParams(vmem_limit_bytes=20 * 2**20),
        )(*parts)

    return jax.shard_map(local_step, mesh=mesh, in_specs=(P('data', None, None, 'model'), P(None, None, 'model', None), P(), P(), P(), P('model', None)), out_specs=P('data', 'model', None, None), check_vma=False)
```

time: 2550 us -> 58.2 us (0.02)
  waiting for transfers between devices: 2180 us -> 0 us
  local copies, waits for them, and re-layouts: 186 us -> 0 us
  matrix products: 75.5 us -> 0 us
  other arithmetic: 69 us -> 0 us
  Pallas kernels: 0 us -> 57 us
  starting transfers between devices: 30.9 us -> 0 us
    all_to_all x3 -> x0, waiting for transfers between devices: 2180 us -> none  [the longest x1 1040 us: local_step(): short_recv = lax.all_to_all(short_part, 'model', 1, 1, tiled=True)]
    convert_element_type x3 -> x0, local copies, waits for them, and re-layouts: 69.4 us -> none  [the longest x2 68.5 us: local_step(): lax.conv_general_dilated(images, w_conv1, (1, 1), 'SAME', dimension_numbe...]
    reshape x2 -> x0, local copies, waits for them, and re-layouts: 68 us -> none  [the longest x1 34.2 us: local_step(): interior = part_sum.reshape(num_images, groups, tile_rows, img_width, c_mid)]
    pallas_call x0 -> x2, Pallas kernels: none -> 57 us  [the longest x1 51.5 us: local_step(): pl.pallas_call(functools.partial(gather_kernel, n), out_shape=[pltpu.VMEM...]
    conv_general_dilated x2 -> x0, matrix products: 51.1 us -> none  [the longest x1 42.3 us: local_step(): lax.conv_general_dilated(images, w_conv1, (1, 1), 'SAME', dimension_numbe...]
    reduce_sum x3 -> x0, other arithmetic: 42.2 us -> none  [the longest x1 19.1 us: local_step(): shortcut = jnp.sum(short_recv, axis=1, dtype=jnp.float32)]
    all_to_all x3 -> x0, starting transfers between devices: 30.9 us -> none  [the longest x1 11.3 us: local_step(): edge_recv = lax.all_to_all(edge_send, 'model', 1, 1, tiled=True)]
  transfers between devices with their start and end apart: 3 -> 0, of which waited for: 3 -> 0; matrix products, arithmetic and copies ran while one was open for 6% -> 0% of each run, Pallas kernels for 0% -> 0%
where the time goes in v2:
time: 58.2 us; the launch traced here: 57 us
  Pallas kernels  57 us (98%)
    pallas_call x1, Pallas kernels, local_step(): pl.pallas_call(functools.partial(gather_kernel, n), out_shape=[pltpu.VMEM...  51.5 us
    pallas_call x1, Pallas kernels, local_step(): pl.pallas_call(functools.partial(finish_kernel, n, height), out_shape=jax...  5.51 us

profile of v2, /device:TPU:21, one launch (start us, length us, event | category | flops | bytes accessed | tf_op | source)
XLA Modules:
  0.0 57.0 jit_solution(14488262118457761232)
XLA Ops:
  0.0 51.5 %shard_map.64 = (bf16[3,16,2,20,4,128]{5,4,3,2,1,0:T(4,128)(2,1)S(1)}, bf16[256,768]{1,0:T(8,128)(2,1)S(1)}, bf16[256,256]{1,0:T(8,128)(2,1)S(1)}, bf16[128,1152...) custom-call(bf16[3,256,4,256]{3,2,1,0:T(4,128)(2,1)} %bitcast.3, ...), custom_call_target="tpu_custom_call" | custom-call | tf_op jit(solution)/shard_map/pallas_call | solution.py:306
  51.5 5.5 %shard_map.65 = f32[3,16,256,128]{3,2,1,0:T(8,128)} custom-call(bf16[3,16,2,20,4,128]{5,4,3,2,1,0:T(4,128)(2,1)S(1)} %get-tuple-element.14.xbuf, bf16[256,768]{1,0:T(8,128)(2,1)S(1)} %get-tuple-element.15.wt, bf16[256,256]{1,0:T(8,128)(2,1)S(1)} %get-tuple-element.16.st, bf16[128,1152]{1,0:T(8,128)(2,1)S(1)} %get-tuple-element.17.w2t, ...), custom_call_target="tpu_custom_call" | custom-call | tf_op jit(solution)/shard_map/pallas_call | solution.py:333

commit v3 on v2

v3 whole, which is shorter than its diff:
```python
import functools

import jax
import jax.numpy as jnp
from jax import lax
from jax.experimental import pallas as pl
from jax.experimental.pallas import tpu as pltpu
from jax.sharding import PartitionSpec as P

MESH = pl.DeviceIdType.MESH
LANES = 128
LATE = 6
SLOT = (0, 2, 1, 3)


def shift_right(v):
    return jnp.concatenate([jnp.zeros((v.shape[0], 1), v.dtype), v[:, :-1]], axis=1)


def shift_left(v):
    return jnp.concatenate([v[:, 1:], jnp.zeros((v.shape[0], 1), v.dtype)], axis=1)


def first_pair(n, height, img, p, xbuf, wt, st, b1c, y1s, sbuf):
    ni, _, rows, halves, ch, _ = xbuf.shape
    tile = rows - 4
    c_mid, c_out = wt.shape[0] // 2, st.shape[0] // 2
    kb = n * 4 * ch
    me = lax.axis_index('model')
    xk = xbuf.reshape(ni, n, rows * halves * ch, LANES)
    two = 2 * halves * ch
    xa = xk[img, :, pl.ds(pl.multiple_of(p * two, two), two), :]
    xb = xk[img, :, pl.ds(pl.multiple_of((p + 1) * two, two), two), :]
    left = lax.broadcasted_iota(jnp.int32, xa.shape, 1) % (2 * ch) < ch
    x_left = jnp.where(left, xa, pltpu.roll(xb, ch, axis=1))
    x_right = jnp.where(left, pltpu.roll(xa, two - ch, axis=1), xb)
    x0 = jnp.concatenate([x_left.reshape(kb, LANES), x_right.reshape(kb, LANES)], axis=1)
    rhs = jnp.concatenate([shift_right(x0), x0, shift_left(x0)], axis=0)
    z2 = jnp.dot(wt[...], rhs, preferred_element_type=jnp.float32)
    s2 = jnp.dot(st[...], x0, preferred_element_type=jnp.float32)
    for a in range(2):
        y = jnp.maximum(z2[a * c_mid:(a + 1) * c_mid] + b1c[:, 0:1], 0.0)
        row = me * tile - 1 + 2 * p + a
        y = jnp.where((row >= 0) & (row < height), y, 0.0).astype(jnp.bfloat16)
        base = pl.multiple_of((2 * p + a) * 3 * c_mid, c_mid)
        y1s[pl.ds(base, c_mid), :] = shift_right(y)
        y1s[pl.ds(base + c_mid, c_mid), :] = y
        y1s[pl.ds(base + 2 * c_mid, c_mid), :] = shift_left(y)
        sbuf[2 * p + a] = s2[a * c_out:(a + 1) * c_out]


def second_row(r, w2t, b2_ref, y1s, sbuf):
    c_mid = w2t.shape[1] // 9
    base = pl.multiple_of(r * 3 * c_mid, c_mid)
    y2 = jnp.dot(w2t[...], y1s[pl.ds(base, 9 * c_mid), :], preferred_element_type=jnp.float32) + sbuf[r + 1]
    return y2.T + b2_ref[...]


def loop(lo, hi, body, unroll=1):
    def step(i, _):
        body(i)
        return 0

    lax.fori_loop(lo, hi, step, 0, unroll=unroll)


def gather_kernel(n, x_ref, w1_ref, b1_hbm, w2_hbm, b2_hbm, ws_ref,
                  xbuf, wt, st, w2t, b1c, b2_ref, y1s, sbuf, y2,
                  gw, gs, wk, sk, w2_ref, b1_ref,
                  local, phase, send_x, recv_x, send_h, recv_h, send_w, recv_w, send_v, recv_v):
    ni, height, halves, ch, _ = x_ref.shape
    tile = height // n
    nz = n // 2
    last = ni - 1
    c_mid, c_out = w1_ref.shape[3], ws_ref.shape[1]
    kb = n * 4 * ch
    me = lax.axis_index('model')
    my_z, my_c = me // 2, me % 2
    sibling = me + 1 - 2 * my_c

    def core(d, c):
        return ((my_z + d) % nz) * 2 + (my_c + c) % 2

    barrier = pltpu.get_barrier_semaphore()
    for dest in (sibling, core(1, 0), core(1, 1), core(nz - 1, 0), core(nz - 1, 1)):
        pl.semaphore_signal(barrier, inc=1, device_id={'model': dest}, device_id_type=MESH)

    block = tile + 2
    inner, outer = (block - LATE, last), (LATE, ni)

    def part_copy(img, dest, odd, part):
        rows, k = part
        base = jnp.clip(dest * tile - 2 * (1 - odd), 0, height - block)
        off = {block: 0, block - LATE: (1 - odd) * LATE, LATE: odd * (block - LATE)}[rows]
        return (x_ref.at[img, pl.ds(base + off, rows)], xbuf.at[img, me, pl.ds(base + off - dest * tile + 2, rows)], recv_x.at[k])

    def parts_of(img):
        return [(block, img)] if img < last else [inner, outer]

    def send(img, hops, parts):
        for part in parts:
            for d in hops:
                for c in range(2) if d else (1,):
                    dest = core(d, c)
                    src, dst, sem = part_copy(img, dest, (my_c + c) % 2, part)
                    pltpu.make_async_remote_copy(src_ref=src, dst_ref=dst, send_sem=send_x, recv_sem=sem,
                                                 device_id={'model': dest}, device_id_type=MESH).start()

    def send_weights(hops):
        for d in hops:
            for k, (src, dst) in enumerate(((w1_ref, gw), (ws_ref, gs))):
                pltpu.make_async_remote_copy(
                    src_ref=src, dst_ref=dst.at[my_z, my_c], send_sem=send_w.at[k], recv_sem=recv_w.at[k],
                    device_id={'model': core(d, 0)}, device_id_type=MESH).start()

    def arrived(ref, sem):
        pltpu.make_async_remote_copy(src_ref=ref, dst_ref=ref, send_sem=send_x, recv_sem=sem,
                                     device_id={'model': sibling}, device_id_type=MESH).wait_recv()

    for img in range(ni):
        for part in parts_of(img):
            src, dst, sem = part_copy(img, me, my_c, part)
            pltpu.make_async_copy(src, dst, sem).start()
    pltpu.make_async_copy(w1_ref, gw.at[my_z, my_c], recv_w.at[0]).start()
    pltpu.make_async_copy(ws_ref, gs.at[my_z, my_c], recv_w.at[1]).start()

    fetches = [pltpu.make_async_copy(src, dst, local.at[k])
               for k, (src, dst) in enumerate(((b1_hbm, b1_ref), (b2_hbm, b2_ref), (w2_hbm, w2_ref)))]
    for fetch in fetches:
        fetch.start()

    pl.semaphore_wait(barrier, 5)
    for d in range(1, nz // 2 + 1):
        if d < nz // 2:
            for side in (1, nz - 1):
                pl.semaphore_signal(phase.at[d - 1], inc=1, device_id={'model': core(side, 0)}, device_id_type=MESH)
        send(0, [d, nz - d] if d < nz // 2 else [d], parts_of(0))
        if d < nz // 2:
            pl.semaphore_wait(phase.at[d - 1], 2)
    send(0, [0], parts_of(0))
    near = [d for k in range(1, nz // 2) for d in (k, nz - k)]
    far = [nz // 2] + near[::-1]
    send_weights(far)
    for img in range(1, ni):
        send(img, far + [0], parts_of(img))

    for owner, r0 in ((0, 0), (n - 1, tile + 2)):
        @pl.when(me == owner)
        def _():
            for img in range(ni):
                xbuf[img, :, r0:r0 + 2] = jnp.zeros((n, 2, halves, ch, LANES), xbuf.dtype)

    for fetch in fetches:
        fetch.wait()
    b1c[...] = jnp.broadcast_to(b1_ref[...], (c_mid, c_mid)).T
    for t in range(9):
        w2t[:, t * c_mid:(t + 1) * c_mid] = w2_ref[t // 3, t % 3].astype(jnp.float32).T.astype(w2t.dtype)
    wk[...] = jnp.zeros_like(wk)
    sk[...] = jnp.zeros_like(sk)

    shares = []
    for k, ref in enumerate((gw.at[:, my_c], gs.at[:, my_c])):
        arrived(ref, recv_w.at[k])
        shares.append(pltpu.make_async_remote_copy(
            src_ref=ref, dst_ref=ref, send_sem=send_v.at[k], recv_sem=recv_v.at[k],
            device_id={'model': sibling}, device_id_type=MESH))
        shares[k].start()
    for share in shares:
        share.wait()

    def place(z):
        for c in range(2):
            src = z * 2 + c
            for dh in range(3):
                for dw in range(3):
                    piece = gw[z, c, dh, dw].astype(jnp.float32)
                    for a in range(2):
                        wk[dw, src, SLOT[dh + a] * ch:(SLOT[dh + a] + 1) * ch, a * c_mid:(a + 1) * c_mid] = piece
            piece = gs[z, c].astype(jnp.float32)
            for a in range(2):
                sk[src, SLOT[1 + a] * ch:(SLOT[1 + a] + 1) * ch, a * c_out:(a + 1) * c_out] = piece

    loop(0, nz, place)
    for dw in range(3):
        wt[:, dw * kb:(dw + 1) * kb] = wk[dw].reshape(kb, 2 * c_mid).T.astype(wt.dtype)
    st[...] = sk[...].reshape(kb, 2 * c_out).T.astype(st.dtype)

    def pair(img, p):
        first_pair(n, height, img, p, xbuf, wt, st, b1c, y1s, sbuf)

    def second(img, r):
        y2[img, r] = second_row(r, w2t, b2_ref, y1s, sbuf)

    def halo(img):
        return pltpu.make_async_remote_copy(
            src_ref=xbuf.at[img, :, pl.ds(2 + (1 - my_c) * (tile - 2), 2)],
            dst_ref=xbuf.at[img, :, pl.ds(my_c * (tile + 2), 2)],
            send_sem=send_h.at[img], recv_sem=recv_h.at[img], device_id={'model': sibling}, device_id_type=MESH)

    sends_halo = (me != 1) & (me != n - 2)
    takes_halo = (me != 0) & (me != n - 1)

    def start_halo(img):
        @pl.when(sends_halo)
        def _():
            halo(img).start()

    def wait_halo(img):
        @pl.when(takes_halo)
        def _():
            halo(img).wait_recv()

    pairs = tile // 2 + 1
    flip = pairs - 1
    for img in range(last):
        arrived(xbuf.at[img, :, pl.ds(0, block)], recv_x.at[img])
        start_halo(img)
        loop(0, pairs - 1, lambda k: pair(img, k + my_c * (flip - 2 * k)))
        wait_halo(img)
        pair(img, (1 - my_c) * flip)
        loop(0, tile, lambda r: second(img, r), unroll=2)

    arrived(xbuf.at[last, :, pl.ds(0, block - LATE)], recv_x.at[last])
    start_halo(last)
    first_p = LATE // 2 + 1
    loop(first_p, pairs - 1, lambda k: pair(last, k + my_c * (flip - 2 * k)))
    wait_halo(last)
    pair(last, (1 - my_c) * flip)
    done = tile - 2 * first_p
    loop(0, done, lambda r: second(last, r + (1 - my_c) * (tile - done)), unroll=2)

    sent = xbuf.at[:, pl.ds(0, n - 1), pl.ds(0, block)]
    pltpu.make_async_remote_copy(src_ref=sent, dst_ref=sent, send_sem=send_x, recv_sem=recv_x.at[0],
                                 device_id={'model': sibling}, device_id_type=MESH).wait_send()
    for k, ref in enumerate((gw.at[pl.ds(0, nz - 1), 0], gs.at[pl.ds(0, nz - 1), 0])):
        pltpu.make_async_remote_copy(src_ref=ref, dst_ref=ref, send_sem=send_w.at[k], recv_sem=recv_w.at[k],
                                     device_id={'model': sibling}, device_id_type=MESH).wait_send()
    @pl.when(sends_halo)
    def _():
        for img in range(ni):
            halo(img).wait_send()

    arrived(xbuf.at[last, :, pl.ds(0, LATE)], recv_x.at[ni])


def finish_kernel(n, height, xbuf, wt, st, w2t, b1c, b2_ref, y1s_in, sbuf_in, y2, out_ref, y1s, sbuf, yb, sem):
    ni, tile = y2.shape[0], y2.shape[1]
    last = ni - 1
    my_c = lax.axis_index('model') % 2
    first_p = LATE // 2 + 1
    left = 2 * first_p
    done = tile - left
    ready = (1 - my_c) * left
    todo = my_c * done
    copies = [pltpu.make_async_copy(y2.at[pl.ds(0, last)], out_ref.at[pl.ds(0, last)], sem.at[0]),
              pltpu.make_async_copy(y2.at[last, pl.ds(ready, done)], out_ref.at[last, pl.ds(ready, done)], sem.at[1])]
    for copy in copies:
        copy.start()
    step = 3 * b1c.shape[0]
    edge = (1 - my_c) * left + my_c * (tile - left)
    y1s[pl.ds(pl.multiple_of(edge * step, step), 2 * step), :] = y1s_in[pl.ds(pl.multiple_of(edge * step, step), 2 * step), :]
    sbuf[pl.ds(edge, 2)] = sbuf_in[pl.ds(edge, 2)]
    flip = tile // 2
    loop(0, first_p, lambda k: first_pair(n, height, last, k + my_c * (flip - 2 * k), xbuf, wt, st, b1c, y1s, sbuf))

    def row(k):
        yb[k] = second_row(k + todo, w2t, b2_ref, y1s, sbuf)
        pltpu.make_async_copy(yb.at[k], out_ref.at[last, k + todo], sem.at[2]).start()

    loop(0, left, row, unroll=2)
    for copy in copies:
        copy.wait()
    pltpu.make_async_copy(yb, out_ref.at[last, pl.ds(todo, left)], sem.at[2]).wait()


def solution(mesh):
    n = mesh.shape['model']

    def local_step(images, w_conv1, b_conv1, w_conv2, b_conv2, w_short):
        ni, height, width, ch = images.shape
        c_mid, c_out = w_conv1.shape[3], w_short.shape[1]
        tile, halves, nz = height // n, width // LANES, n // 2
        kb = n * 4 * ch
        x = images.transpose(0, 1, 3, 2).reshape(ni, height, ch, halves, LANES).transpose(0, 1, 3, 2, 4)
        vmem = pl.BlockSpec(memory_space=pltpu.VMEM)
        hbm = pl.BlockSpec(memory_space=pltpu.HBM)
        dma = pltpu.SemaphoreType.DMA
        y1s = pltpu.VMEM(((tile + 2) * 3 * c_mid, width), jnp.bfloat16)
        sbuf = pltpu.VMEM((tile + 2, c_out, width), jnp.float32)
        parts = pl.pallas_call(
            functools.partial(gather_kernel, n),
            out_shape=[
                pltpu.VMEM((ni, n, tile + 4, halves, ch, LANES), jnp.bfloat16),
                pltpu.VMEM((2 * c_mid, 3 * kb), jnp.bfloat16),
                pltpu.VMEM((2 * c_out, kb), jnp.bfloat16),
                pltpu.VMEM((c_out, 9 * c_mid), jnp.bfloat16),
                pltpu.VMEM((c_mid, c_mid), jnp.float32),
                pltpu.VMEM((1, c_out), jnp.float32),
                y1s,
                sbuf,
                pltpu.VMEM((ni, tile, width, c_out), jnp.float32),
            ],
            in_specs=[hbm] * 6,
            out_specs=[vmem] * 9,
            scratch_shapes=[
                pltpu.VMEM((nz, 2, 3, 3, ch, c_mid), jnp.bfloat16),
                pltpu.VMEM((nz, 2, ch, c_out), jnp.bfloat16),
                pltpu.VMEM((3, n, 4 * ch, 2 * c_mid), jnp.float32),
                pltpu.VMEM((n, 4 * ch, 2 * c_out), jnp.float32),
                pltpu.VMEM(w_conv2.shape, w_conv2.dtype),
                pltpu.VMEM((1, c_mid), jnp.float32),
                dma((3,)), pltpu.SemaphoreType.REGULAR((nz // 2,)),
                dma, dma((ni + 1,)), dma((ni,)), dma((ni,)), dma((2,)), dma((2,)), dma((2,)), dma((2,)),
            ],
            compiler_params=pltpu.CompilerParams(collective_id=0, has_side_effects=True, vmem_limit_bytes=20 * 2**20),
        )(*[pltpu.with_memory_space_constraint(v, pltpu.HBM) for v in (x, w_conv1, b_conv1.reshape(1, c_mid), w_conv2, b_conv2.reshape(1, c_out), w_short)])
        return pl.pallas_call(
            functools.partial(finish_kernel, n, height),
            out_shape=jax.ShapeDtypeStruct((ni, tile, width, c_out), jnp.float32),
            in_specs=[vmem] * 9,
            out_specs=hbm,
            scratch_shapes=[y1s, sbuf, pltpu.VMEM((LATE + 2, width, c_out), jnp.float32), dma((3,))],
            compiler_params=pltpu.CompilerParams(vmem_limit_bytes=20 * 2**20),
        )(*parts)

    return jax.shard_map(local_step, mesh=mesh, in_specs=(P('data', None, None, 'model'), P(None, None, 'model', None), P(), P(), P(), P('model', None)), out_specs=P('data', 'model', None, None), check_vma=False)
```

time: 58.2 us -> 56.5 us (0.971); the launches traced: 57 us -> 56.4 us
  Pallas kernels: 57 us -> 56.4 us
    pallas_call x1, Pallas kernels: 5.51 us -> 4.3 us  [local_step(): pl.pallas_call(functools.partial(finish_kernel, n, height), out_shape=jax...]
where the time goes in v3:
time: 56.5 us; the launch traced here: 56.4 us
  Pallas kernels  56.4 us (100%)
    pallas_call x1, Pallas kernels, local_step(): pl.pallas_call(functools.partial(gather_kernel, n), out_shape=[pltpu.VMEM...  52.1 us
    pallas_call x1, Pallas kernels, local_step(): pl.pallas_call(functools.partial(finish_kernel, n, height), out_shape=jax...  4.3 us

profile of v3, /device:TPU:21, one launch (start us, length us, event | category | flops | bytes accessed | tf_op | source)
XLA Modules:
  0.0 56.4 jit_solution(3188660372365431372)
XLA Ops:
  0.0 52.1 %shard_map.64 = (bf16[3,16,20,2,4,128]{5,4,3,2,1,0:T(4,128)(2,1)S(1)}, bf16[256,768]{1,0:T(8,128)(2,1)S(1)}, bf16[256,256]{1,0:T(8,128)(2,1)S(1)}, bf16[128,1152...) custom-call(bf16[3,256,2,4,128]{4,3,2,1,0:T(4,128)(2,1)} %bitcast.7,, ...), custom_call_target="tpu_custom_call" | custom-call | tf_op jit(solution)/shard_map/pallas_call | solution.py:290
  52.1 4.3 %shard_map.65 = f32[3,16,256,128]{3,2,1,0:T(8,128)} custom-call(bf16[3,16,20,2,4,128]{5,4,3,2,1,0:T(4,128)(2,1)S(1)} %get-tuple-element.14.xbuf, bf16[256,768]{1,0:T(8,128)(2,1)S(1)} %get-tuple-element.15.wt, bf16[256,256]{1,0:T(8,128)(2,1)S(1)} %get-tuple-element.16.st, bf16[128,1152]{1,0:T(8,128)(2,1)S(1)} %get-tuple-element.17.w2t, ...), custom_call_target="tpu_custom_call" | custom-call | tf_op jit(solution)/shard_map/pallas_call | solution.py:317

commit v4 on v3

--- a/solution.py
+++ b/solution.py
@@ -10,15 +10,16 @@
 MESH = pl.DeviceIdType.MESH
 LANES = 128
 LATE = 6
-SLOT = (0, 2, 1, 3)
 
 
 def shift_right(v):
-    return jnp.concatenate([jnp.zeros((v.shape[0], 1), v.dtype), v[:, :-1]], axis=1)
+    first = lax.broadcasted_iota(jnp.int32, v.shape, 1) == 0
+    return jnp.where(first, jnp.zeros_like(v), pltpu.roll(v, 1, axis=1))
 
 
 def shift_left(v):
-    return jnp.concatenate([v[:, 1:], jnp.zeros((v.shape[0], 1), v.dtype)], axis=1)
+    last = lax.broadcasted_iota(jnp.int32, v.shape, 1) == v.shape[1] - 1
+    return jnp.where(last, jnp.zeros_like(v), pltpu.roll(v, v.shape[1] - 1, axis=1))
 
 
 def first_pair(n, height, img, p, xbuf, wt, st, b1c, y1s, sbuf):
@@ -27,19 +28,14 @@
     c_mid, c_out = wt.shape[0] // 2, st.shape[0] // 2
     kb = n * 4 * ch
     me = lax.axis_index('model')
-    xk = xbuf.reshape(ni, n, rows * halves * ch, LANES)
-    two = 2 * halves * ch
-    xa = xk[img, :, pl.ds(pl.multiple_of(p * two, two), two), :]
-    xb = xk[img, :, pl.ds(pl.multiple_of((p + 1) * two, two), two), :]
-    left = lax.broadcasted_iota(jnp.int32, xa.shape, 1) % (2 * ch) < ch
-    x_left = jnp.where(left, xa, pltpu.roll(xb, ch, axis=1))
-    x_right = jnp.where(left, pltpu.roll(xa, two - ch, axis=1), xb)
+    x_left = xbuf[img, :, pl.ds(2 * p, 4), 0]
+    x_right = xbuf[img, :, pl.ds(2 * p, 4), 1]
     x0 = jnp.concatenate([x_left.reshape(kb, LANES), x_right.reshape(kb, LANES)], axis=1)
     rhs = jnp.concatenate([shift_right(x0), x0, shift_left(x0)], axis=0)
     z2 = jnp.dot(wt[...], rhs, preferred_element_type=jnp.float32)
     s2 = jnp.dot(st[...], x0, preferred_element_type=jnp.float32)
     for a in range(2):
-        y = jnp.maximum(z2[a * c_mid:(a + 1) * c_mid] + b1c[:, 0:1], 0.0)
+        y = jnp.maximum(z2[a * c_mid:(a + 1) * c_mid] + jnp.concatenate([b1c[...]] * halves, axis=1), 0.0)
         row = me * tile - 1 + 2 * p + a
         y = jnp.where((row >= 0) & (row < height), y, 0.0).astype(jnp.bfloat16)
         base = pl.multiple_of((2 * p + a) * 3 * c_mid, c_mid)
@@ -152,7 +148,7 @@
 
     for fetch in fetches:
         fetch.wait()
-    b1c[...] = jnp.broadcast_to(b1_ref[...], (c_mid, c_mid)).T
+    b1c[...] = jnp.broadcast_to(b1_ref[...], (LANES, c_mid)).T
     for t in range(9):
         w2t[:, t * c_mid:(t + 1) * c_mid] = w2_ref[t // 3, t % 3].astype(jnp.float32).T.astype(w2t.dtype)
     wk[...] = jnp.zeros_like(wk)
@@ -175,10 +171,10 @@
                 for dw in range(3):
                     piece = gw[z, c, dh, dw].astype(jnp.float32)
                     for a in range(2):
-                        wk[dw, src, SLOT[dh + a] * ch:(SLOT[dh + a] + 1) * ch, a * c_mid:(a + 1) * c_mid] = piece
+                        wk[dw, src, (dh + a) * ch:(dh + a + 1) * ch, a * c_mid:(a + 1) * c_mid] = piece
             piece = gs[z, c].astype(jnp.float32)
             for a in range(2):
-                sk[src, SLOT[1 + a] * ch:(SLOT[1 + a] + 1) * ch, a * c_out:(a + 1) * c_out] = piece
+                sk[src, (1 + a) * ch:(2 + a) * ch, a * c_out:(a + 1) * c_out] = piece
 
     loop(0, nz, place)
     for dw in range(3):
@@ -215,19 +211,19 @@
     for img in range(last):
         arrived(xbuf.at[img, :, pl.ds(0, block)], recv_x.at[img])
         start_halo(img)
-        loop(0, pairs - 1, lambda k: pair(img, k + my_c * (flip - 2 * k)))
+        loop(0, pairs - 1, lambda k: pair(img, k + my_c * (flip - 2 * k)), unroll=4)
         wait_halo(img)
         pair(img, (1 - my_c) * flip)
-        loop(0, tile, lambda r: second(img, r), unroll=2)
+        loop(0, tile, lambda r: second(img, r), unroll=4)
 
     arrived(xbuf.at[last, :, pl.ds(0, block - LATE)], recv_x.at[last])
     start_halo(last)
     first_p = LATE // 2 + 1
-    loop(first_p, pairs - 1, lambda k: pair(last, k + my_c * (flip - 2 * k)))
+    loop(first_p, pairs - 1, lambda k: pair(last, k + my_c * (flip - 2 * k)), unroll=4)
     wait_halo(last)
     pair(last, (1 - my_c) * flip)
     done = tile - 2 * first_p
-    loop(0, done, lambda r: second(last, r + (1 - my_c) * (tile - done)), unroll=2)
+    loop(0, done, lambda r: second(last, r + (1 - my_c) * (tile - done)), unroll=4)
 
     sent = xbuf.at[:, pl.ds(0, n - 1), pl.ds(0, block)]
     pltpu.make_async_remote_copy(src_ref=sent, dst_ref=sent, send_sem=send_x, recv_sem=recv_x.at[0],
@@ -261,13 +257,13 @@
     y1s[pl.ds(pl.multiple_of(edge * step, step), 2 * step), :] = y1s_in[pl.ds(pl.multiple_of(edge * step, step), 2 * step), :]
     sbuf[pl.ds(edge, 2)] = sbuf_in[pl.ds(edge, 2)]
     flip = tile // 2
-    loop(0, first_p, lambda k: first_pair(n, height, last, k + my_c * (flip - 2 * k), xbuf, wt, st, b1c, y1s, sbuf))
+    loop(0, first_p, lambda k: first_pair(n, height, last, k + my_c * (flip - 2 * k), xbuf, wt, st, b1c, y1s, sbuf), unroll=4)
 
     def row(k):
         yb[k] = second_row(k + todo, w2t, b2_ref, y1s, sbuf)
         pltpu.make_async_copy(yb.at[k], out_ref.at[last, k + todo], sem.at[2]).start()
 
-    loop(0, left, row, unroll=2)
+    loop(0, left, row, unroll=8)
     for copy in copies:
         copy.wait()
     pltpu.make_async_copy(yb, out_ref.at[last, pl.ds(todo, left)], sem.at[2]).wait()
@@ -294,7 +290,7 @@
                 pltpu.VMEM((2 * c_mid, 3 * kb), jnp.bfloat16),
                 pltpu.VMEM((2 * c_out, kb), jnp.bfloat16),
                 pltpu.VMEM((c_out, 9 * c_mid), jnp.bfloat16),
-                pltpu.VMEM((c_mid, c_mid), jnp.float32),
+                pltpu.VMEM((c_mid, LANES), jnp.float32),
                 pltpu.VMEM((1, c_out), jnp.float32),
                 y1s,
                 sbuf,

time: 56.5 us -> 54.9 us (0.972)
  Pallas kernels: 56.4 us -> 54.8 us
    pallas_call x1, Pallas kernels: 52.1 us -> 50.8 us  [local_step(): pl.pallas_call(functools.partial(gather_kernel, n), out_shape=[pltpu.VMEM...]
where the time goes in v4:
time: 54.9 us; the launch traced here: 54.8 us
  Pallas kernels  54.8 us (100%)
    pallas_call x1, Pallas kernels, local_step(): pl.pallas_call(functools.partial(gather_kernel, n), out_shape=[pltpu.VMEM...  50.8 us
    pallas_call x1, Pallas kernels, local_step(): pl.pallas_call(functools.partial(finish_kernel, n, height), out_shape=jax...  3.96 us

profile of v4, /device:TPU:21, one launch (start us, length us, event | category | flops | bytes accessed | tf_op | source)
XLA Modules:
  0.0 54.8 jit_solution(10899291758582845837)
XLA Ops:
  0.0 50.8 %shard_map.64 = (bf16[3,16,20,2,4,128]{5,4,3,2,1,0:T(4,128)(2,1)S(1)}, bf16[256,768]{1,0:T(8,128)(2,1)S(1)}, bf16[256,256]{1,0:T(8,128)(2,1)S(1)}, bf16[128,1152...) custom-call(bf16[3,256,2,4,128]{4,3,2,1,0:T(4,128)(2,1)} %bitcast.7,, ...), custom_call_target="tpu_custom_call" | custom-call | tf_op jit(solution)/shard_map/pallas_call | solution.py:286
  50.8 4.0 %shard_map.65 = f32[3,16,256,128]{3,2,1,0:T(8,128)} custom-call(bf16[3,16,20,2,4,128]{5,4,3,2,1,0:T(4,128)(2,1)S(1)} %get-tuple-element.14.xbuf, bf16[256,768]{1,0:T(8,128)(2,1)S(1)} %get-tuple-element.15.wt, bf16[256,256]{1,0:T(8,128)(2,1)S(1)} %get-tuple-element.16.st, bf16[128,1152]{1,0:T(8,128)(2,1)S(1)} %get-tuple-element.17.w2t, ...), custom_call_target="tpu_custom_call" | custom-call | tf_op jit(solution)/shard_map/pallas_call | solution.py:313

commit v5 on v4

--- a/solution.py
+++ b/solution.py
@@ -86,12 +86,15 @@
 
     def part_copy(img, dest, odd, part):
         rows, k = part
-        base = jnp.clip(dest * tile - 2 * (1 - odd), 0, height - block)
-        off = {block: 0, block - LATE: (1 - odd) * LATE, LATE: odd * (block - LATE)}[rows]
+        if img < last:
+            base, off = dest * tile, 0
+        else:
+            base = jnp.clip(dest * tile - 2 * (1 - odd), 0, height - block)
+            off = (1 - odd) * LATE if part is inner else odd * (block - LATE)
         return (x_ref.at[img, pl.ds(base + off, rows)], xbuf.at[img, me, pl.ds(base + off - dest * tile + 2, rows)], recv_x.at[k])
 
     def parts_of(img):
-        return [(block, img)] if img < last else [inner, outer]
+        return [(tile, img)] if img < last else [inner, outer]
 
     def send(img, hops, parts):
         for part in parts:
@@ -99,7 +102,7 @@
                 for c in range(2) if d else (1,):
                     dest = core(d, c)
                     src, dst, sem = part_copy(img, dest, (my_c + c) % 2, part)
-                    pltpu.make_async_remote_copy(src_ref=src, dst_ref=dst, send_sem=send_x, recv_sem=sem,
+                    pltpu.make_async_remote_copy(src_ref=src, dst_ref=dst, send_sem=send_x.at[img // last], recv_sem=sem,
                                                  device_id={'model': dest}, device_id_type=MESH).start()
 
     def send_weights(hops):
@@ -110,7 +113,7 @@
                     device_id={'model': core(d, 0)}, device_id_type=MESH).start()
 
     def arrived(ref, sem):
-        pltpu.make_async_remote_copy(src_ref=ref, dst_ref=ref, send_sem=send_x, recv_sem=sem,
+        pltpu.make_async_remote_copy(src_ref=ref, dst_ref=ref, send_sem=send_x.at[0], recv_sem=sem,
                                      device_id={'model': sibling}, device_id_type=MESH).wait_recv()
 
     for img in range(ni):
@@ -137,7 +140,7 @@
     near = [d for k in range(1, nz // 2) for d in (k, nz - k)]
     far = [nz // 2] + near[::-1]
     send_weights(far)
-    for img in range(1, ni):
+    for img in range(1, last):
         send(img, far + [0], parts_of(img))
 
     for owner, r0 in ((0, 0), (n - 1, tile + 2)):
@@ -154,88 +157,113 @@
     wk[...] = jnp.zeros_like(wk)
     sk[...] = jnp.zeros_like(sk)
 
-    shares = []
-    for k, ref in enumerate((gw.at[:, my_c], gs.at[:, my_c])):
-        arrived(ref, recv_w.at[k])
-        shares.append(pltpu.make_async_remote_copy(
-            src_ref=ref, dst_ref=ref, send_sem=send_v.at[k], recv_sem=recv_v.at[k],
-            device_id={'model': sibling}, device_id_type=MESH))
-        shares[k].start()
-    for share in shares:
-        share.wait()
-
-    def place(z):
-        for c in range(2):
-            src = z * 2 + c
-            for dh in range(3):
-                for dw in range(3):
-                    piece = gw[z, c, dh, dw].astype(jnp.float32)
-                    for a in range(2):
-                        wk[dw, src, (dh + a) * ch:(dh + a + 1) * ch, a * c_mid:(a + 1) * c_mid] = piece
-            piece = gs[z, c].astype(jnp.float32)
-            for a in range(2):
-                sk[src, (1 + a) * ch:(2 + a) * ch, a * c_out:(a + 1) * c_out] = piece
-
-    loop(0, nz, place)
-    for dw in range(3):
-        wt[:, dw * kb:(dw + 1) * kb] = wk[dw].reshape(kb, 2 * c_mid).T.astype(wt.dtype)
-    st[...] = sk[...].reshape(kb, 2 * c_out).T.astype(st.dtype)
-
     def pair(img, p):
         first_pair(n, height, img, p, xbuf, wt, st, b1c, y1s, sbuf)
 
     def second(img, r):
         y2[img, r] = second_row(r, w2t, b2_ref, y1s, sbuf)
 
-    def halo(img):
+    def build_weights():
+        shares = []
+        for k, ref in enumerate((gw.at[:, my_c], gs.at[:, my_c])):
+            arrived(ref, recv_w.at[k])
+            shares.append(pltpu.make_async_remote_copy(
+                src_ref=ref, dst_ref=ref, send_sem=send_v.at[k], recv_sem=recv_v.at[k],
+                device_id={'model': sibling}, device_id_type=MESH))
+            shares[k].start()
+        for share in shares:
+            share.wait()
+
+        def place(z):
+            for c in range(2):
+                src = z * 2 + c
+                for dh in range(3):
+                    for dw in range(3):
+                        piece = gw[z, c, dh, dw].astype(jnp.float32)
+                        for a in range(2):
+                            wk[dw, src, (dh + a) * ch:(dh + a + 1) * ch, a * c_mid:(a + 1) * c_mid] = piece
+                piece = gs[z, c].astype(jnp.float32)
+                for a in range(2):
+                    sk[src, (1 + a) * ch:(2 + a) * ch, a * c_out:(a + 1) * c_out] = piece
+
+        loop(0, nz, place)
+        for dw in range(3):
+            wt[:, dw * kb:(dw + 1) * kb] = wk[dw].reshape(kb, 2 * c_mid).T.astype(wt.dtype)
+        st[...] = sk[...].reshape(kb, 2 * c_out).T.astype(st.dtype)
+
+    def inner_halo(img):
         return pltpu.make_async_remote_copy(
             src_ref=xbuf.at[img, :, pl.ds(2 + (1 - my_c) * (tile - 2), 2)],
             dst_ref=xbuf.at[img, :, pl.ds(my_c * (tile + 2), 2)],
-            send_sem=send_h.at[img], recv_sem=recv_h.at[img], device_id={'model': sibling}, device_id_type=MESH)
-
-    sends_halo = (me != 1) & (me != n - 2)
-    takes_halo = (me != 0) & (me != n - 1)
-
-    def start_halo(img):
-        @pl.when(sends_halo)
+            send_sem=send_h.at[img, 0], recv_sem=recv_h.at[img, 0], device_id={'model': sibling}, device_id_type=MESH)
+
+    def outer_halo(img):
+        return pltpu.make_async_remote_copy(
+            src_ref=xbuf.at[img, :, pl.ds(2 + my_c * (tile - 2), 2)],
+            dst_ref=xbuf.at[img, :, pl.ds((1 - my_c) * (tile + 2), 2)],
+            send_sem=send_h.at[img, 1], recv_sem=recv_h.at[img, 1],
+            device_id={'model': (me + n - 1 + 2 * my_c) % n}, device_id_type=MESH)
+
+    has_outer = (me != 0) & (me != n - 1)
+    sends_last = (me != 1) & (me != n - 2)
+
+    def when(cond, act):
+        @pl.when(cond)
         def _():
-            halo(img).start()
-
-    def wait_halo(img):
-        @pl.when(takes_halo)
-        def _():
-            halo(img).wait_recv()
-
-    pairs = tile // 2 + 1
-    flip = pairs - 1
+            act()
+
+    flip = tile // 2
+
+    def pair_in(img, k):
+        pair(img, k + my_c * (flip - 2 * k))
+
+    def rows_in(img, lo, hi, unroll):
+        loop(lo, hi, lambda k: second(img, k + my_c * (tile - 1 - 2 * k)), unroll=unroll)
+
+    def most(img):
+        loop(1, flip - 1, lambda k: pair_in(img, k), unroll=3)
+        inner_halo(img).wait_recv()
+        loop(flip - 1, flip + 1, lambda k: pair_in(img, k), unroll=2)
+        rows_in(img, 2, tile, 7)
+
+    def edge(img):
+        when(has_outer, lambda: outer_halo(img).wait_recv())
+        pair_in(img, 0)
+        rows_in(img, 0, 2, 2)
+
     for img in range(last):
-        arrived(xbuf.at[img, :, pl.ds(0, block)], recv_x.at[img])
-        start_halo(img)
-        loop(0, pairs - 1, lambda k: pair(img, k + my_c * (flip - 2 * k)), unroll=4)
-        wait_halo(img)
-        pair(img, (1 - my_c) * flip)
-        loop(0, tile, lambda r: second(img, r), unroll=4)
+        arrived(xbuf.at[img, :, pl.ds(0, tile)], recv_x.at[img])
+        inner_halo(img).start()
+        when(has_outer, lambda: outer_halo(img).start())
+        if img == last - 2:
+            send(last, far + [0], [inner])
+        if img == last - 1:
+            send(last, far + [0], [outer] if last > 1 else [inner, outer])
+        if img == 0:
+            build_weights()
+        else:
+            edge(img - 1)
+        most(img)
 
     arrived(xbuf.at[last, :, pl.ds(0, block - LATE)], recv_x.at[last])
-    start_halo(last)
+    when(sends_last, lambda: inner_halo(last).start())
+    edge(last - 1)
     first_p = LATE // 2 + 1
-    loop(first_p, pairs - 1, lambda k: pair(last, k + my_c * (flip - 2 * k)), unroll=4)
-    wait_halo(last)
-    pair(last, (1 - my_c) * flip)
-    done = tile - 2 * first_p
-    loop(0, done, lambda r: second(last, r + (1 - my_c) * (tile - done)), unroll=4)
-
-    sent = xbuf.at[:, pl.ds(0, n - 1), pl.ds(0, block)]
-    pltpu.make_async_remote_copy(src_ref=sent, dst_ref=sent, send_sem=send_x, recv_sem=recv_x.at[0],
-                                 device_id={'model': sibling}, device_id_type=MESH).wait_send()
+    loop(first_p, flip - 1, lambda k: pair_in(last, k), unroll=3)
+    when(has_outer, lambda: inner_halo(last).wait_recv())
+    loop(flip - 1, flip + 1, lambda k: pair_in(last, k), unroll=2)
+    rows_in(last, 2 * first_p, tile, 4)
+
+    for k, sent in enumerate((xbuf.at[pl.ds(0, last), pl.ds(0, n - 1), pl.ds(0, tile)], xbuf.at[last, pl.ds(0, n - 1), pl.ds(0, block)])):
+        pltpu.make_async_remote_copy(src_ref=sent, dst_ref=sent, send_sem=send_x.at[k], recv_sem=recv_x.at[0],
+                                     device_id={'model': sibling}, device_id_type=MESH).wait_send()
     for k, ref in enumerate((gw.at[pl.ds(0, nz - 1), 0], gs.at[pl.ds(0, nz - 1), 0])):
         pltpu.make_async_remote_copy(src_ref=ref, dst_ref=ref, send_sem=send_w.at[k], recv_sem=recv_w.at[k],
                                      device_id={'model': sibling}, device_id_type=MESH).wait_send()
-    @pl.when(sends_halo)
-    def _():
-        for img in range(ni):
-            halo(img).wait_send()
-
+    for img in range(last):
+        inner_halo(img).wait_send()
+        when(has_outer, lambda: outer_halo(img).wait_send())
+    when(sends_last, lambda: inner_halo(last).wait_send())
     arrived(xbuf.at[last, :, pl.ds(0, LATE)], recv_x.at[ni])
 
 
@@ -248,8 +276,9 @@
     done = tile - left
     ready = (1 - my_c) * left
     todo = my_c * done
-    copies = [pltpu.make_async_copy(y2.at[pl.ds(0, last)], out_ref.at[pl.ds(0, last)], sem.at[0]),
-              pltpu.make_async_copy(y2.at[last, pl.ds(ready, done)], out_ref.at[last, pl.ds(ready, done)], sem.at[1])]
+    copies = [pltpu.make_async_copy(y2.at[img, pl.ds(r, 4)], out_ref.at[img, pl.ds(r, 4)], sem.at[0])
+              for img in range(last) for r in range(0, tile, 4)]
+    copies += [pltpu.make_async_copy(y2.at[last, pl.ds(ready, done)], out_ref.at[last, pl.ds(ready, done)], sem.at[1])]
     for copy in copies:
         copy.start()
     step = 3 * b1c.shape[0]
@@ -257,13 +286,13 @@
     y1s[pl.ds(pl.multiple_of(edge * step, step), 2 * step), :] = y1s_in[pl.ds(pl.multiple_of(edge * step, step), 2 * step), :]
     sbuf[pl.ds(edge, 2)] = sbuf_in[pl.ds(edge, 2)]
     flip = tile // 2
-    loop(0, first_p, lambda k: first_pair(n, height, last, k + my_c * (flip - 2 * k), xbuf, wt, st, b1c, y1s, sbuf), unroll=4)
+    loop(0, first_p, lambda k: first_pair(n, height, last, k + my_c * (flip - 2 * k), xbuf, wt, st, b1c, y1s, sbuf), unroll=2)
 
     def row(k):
         yb[k] = second_row(k + todo, w2t, b2_ref, y1s, sbuf)
         pltpu.make_async_copy(yb.at[k], out_ref.at[last, k + todo], sem.at[2]).start()
 
-    loop(0, left, row, unroll=8)
+    loop(0, left, row, unroll=4)
     for copy in copies:
         copy.wait()
     pltpu.make_async_copy(yb, out_ref.at[last, pl.ds(todo, left)], sem.at[2]).wait()
@@ -306,7 +335,7 @@
                 pltpu.VMEM(w_conv2.shape, w_conv2.dtype),
                 pltpu.VMEM((1, c_mid), jnp.float32),
                 dma((3,)), pltpu.SemaphoreType.REGULAR((nz // 2,)),
-                dma, dma((ni + 1,)), dma((ni,)), dma((ni,)), dma((2,)), dma((2,)), dma((2,)), dma((2,)),
+                dma((2,)), dma((ni + 1,)), dma((ni, 2)), dma((ni, 2)), dma((2,)), dma((2,)), dma((2,)), dma((2,)),
             ],
             compiler_params=pltpu.CompilerParams(collective_id=0, has_side_effects=True, vmem_limit_bytes=20 * 2**20),
         )(*[pltpu.with_memory_space_constraint(v, pltpu.HBM) for v in (x, w_conv1, b_conv1.reshape(1, c_mid), w_conv2, b_conv2.reshape(1, c_out), w_short)])

time: 54.9 us -> 53 us (0.965)
  Pallas kernels: 54.8 us -> 52.6 us
    pallas_call x1, Pallas kernels: 50.8 us -> 49.3 us  [local_step(): pl.pallas_call(functools.partial(gather_kernel, n), out_shape=[pltpu.VMEM...]
    pallas_call x1, Pallas kernels: 3.96 us -> 3.27 us  [local_step(): pl.pallas_call(functools.partial(finish_kernel, n, height), out_shape=jax...]
where the time goes in v5:
time: 53 us; the launch traced here: 52.6 us
  Pallas kernels  52.6 us (99%)
    pallas_call x1, Pallas kernels, local_step(): pl.pallas_call(functools.partial(gather_kernel, n), out_shape=[pltpu.VMEM...  49.3 us
    pallas_call x1, Pallas kernels, local_step(): pl.pallas_call(functools.partial(finish_kernel, n, height), out_shape=jax...  3.27 us

profile of v5, /device:TPU:21, one launch (start us, length us, event | category | flops | bytes accessed | tf_op | source)
XLA Modules:
  0.0 52.6 jit_solution(5446970983706161920)
XLA Ops:
  0.0 49.3 %shard_map.64 = (bf16[3,16,20,2,4,128]{5,4,3,2,1,0:T(4,128)(2,1)S(1)}, bf16[256,768]{1,0:T(8,128)(2,1)S(1)}, bf16[256,256]{1,0:T(8,128)(2,1)S(1)}, bf16[128,1152...) custom-call(bf16[3,256,2,4,128]{4,3,2,1,0:T(4,128)(2,1)} %bitcast.7,, ...), custom_call_target="tpu_custom_call" | custom-call | tf_op jit(solution)/shard_map/pallas_call | solution.py:315
  49.3 3.3 %shard_map.65 = f32[3,16,256,128]{3,2,1,0:T(8,128)} custom-call(bf16[3,16,20,2,4,128]{5,4,3,2,1,0:T(4,128)(2,1)S(1)} %get-tuple-element.14.xbuf, bf16[256,768]{1,0:T(8,128)(2,1)S(1)} %get-tuple-element.15.wt, bf16[256,256]{1,0:T(8,128)(2,1)S(1)} %get-tuple-element.16.st, bf16[128,1152]{1,0:T(8,128)(2,1)S(1)} %get-tuple-element.17.w2t, ...), custom_call_target="tpu_custom_call" | custom-call | tf_op jit(solution)/shard_map/pallas_call | solution.py:342

commit v6 on v5

--- a/solution.py
+++ b/solution.py
@@ -22,10 +22,10 @@
     return jnp.where(last, jnp.zeros_like(v), pltpu.roll(v, v.shape[1] - 1, axis=1))
 
 
-def first_pair(n, height, img, p, xbuf, wt, st, b1c, y1s, sbuf):
+def first_pair(n, height, img, p, xbuf, wt, b1c, y1s):
     ni, _, rows, halves, ch, _ = xbuf.shape
     tile = rows - 4
-    c_mid, c_out = wt.shape[0] // 2, st.shape[0] // 2
+    c_mid = wt.shape[0] // 2
     kb = n * 4 * ch
     me = lax.axis_index('model')
     x_left = xbuf[img, :, pl.ds(2 * p, 4), 0]
@@ -33,7 +33,6 @@
     x0 = jnp.concatenate([x_left.reshape(kb, LANES), x_right.reshape(kb, LANES)], axis=1)
     rhs = jnp.concatenate([shift_right(x0), x0, shift_left(x0)], axis=0)
     z2 = jnp.dot(wt[...], rhs, preferred_element_type=jnp.float32)
-    s2 = jnp.dot(st[...], x0, preferred_element_type=jnp.float32)
     for a in range(2):
         y = jnp.maximum(z2[a * c_mid:(a + 1) * c_mid] + jnp.concatenate([b1c[...]] * halves, axis=1), 0.0)
         row = me * tile - 1 + 2 * p + a
@@ -42,13 +41,15 @@
         y1s[pl.ds(base, c_mid), :] = shift_right(y)
         y1s[pl.ds(base + c_mid, c_mid), :] = y
         y1s[pl.ds(base + 2 * c_mid, c_mid), :] = shift_left(y)
-        sbuf[2 * p + a] = s2[a * c_out:(a + 1) * c_out]
-
-
-def second_row(r, w2t, b2_ref, y1s, sbuf):
-    c_mid = w2t.shape[1] // 9
+
+
+def second_row(img, r, xbuf, w2x, b2_ref, y1s):
+    _, n, _, halves, ch, _ = xbuf.shape
+    c_mid = w2x.shape[0]
     base = pl.multiple_of(r * 3 * c_mid, c_mid)
-    y2 = jnp.dot(w2t[...], y1s[pl.ds(base, 9 * c_mid), :], preferred_element_type=jnp.float32) + sbuf[r + 1]
+    x_row = jnp.concatenate([xbuf[img, :, r + 2, h].reshape(n * ch, LANES) for h in range(halves)], axis=1)
+    rhs = jnp.concatenate([y1s[pl.ds(base, 9 * c_mid), :], x_row], axis=0)
+    y2 = jnp.dot(w2x[...], rhs, preferred_element_type=jnp.float32)
     return y2.T + b2_ref[...]
 
 
@@ -61,8 +62,8 @@
 
 
 def gather_kernel(n, x_ref, w1_ref, b1_hbm, w2_hbm, b2_hbm, ws_ref,
-                  xbuf, wt, st, w2t, b1c, b2_ref, y1s, sbuf, y2,
-                  gw, gs, wk, sk, w2_ref, b1_ref,
+                  xbuf, wt, w2x, b1c, b2_ref, y1s, y2,
+                  gw, gs, wk, w2_ref, b1_ref,
                   local, phase, send_x, recv_x, send_h, recv_h, send_w, recv_w, send_v, recv_v):
     ni, height, halves, ch, _ = x_ref.shape
     tile = height // n
@@ -105,12 +106,21 @@
                     pltpu.make_async_remote_copy(src_ref=src, dst_ref=dst, send_sem=send_x.at[img // last], recv_sem=sem,
                                                  device_id={'model': dest}, device_id_type=MESH).start()
 
-    def send_weights(hops):
-        for d in hops:
+    hubs = [2, nz - 2] if nz >= 8 else [d for d in range(1, nz)]
+
+    own = 0
+
+    def send_weights(moves, k_sem):
+        for off, d in moves:
             for k, (src, dst) in enumerate(((w1_ref, gw), (ws_ref, gs))):
+                piece = dst.at[(my_z + off) % nz, my_c]
                 pltpu.make_async_remote_copy(
-                    src_ref=src, dst_ref=dst.at[my_z, my_c], send_sem=send_w.at[k], recv_sem=recv_w.at[k],
+                    src_ref=src if off is own else piece, dst_ref=piece, send_sem=send_w.at[k], recv_sem=recv_w.at[k, k_sem],
                     device_id={'model': core(d, 0)}, device_id_type=MESH).start()
+
+    def wait_weights(pieces, k_sem):
+        for k, ref in enumerate((gw, gs)):
+            arrived(ref.at[pl.ds(0, pieces), my_c], recv_w.at[k, k_sem])
 
     def arrived(ref, sem):
         pltpu.make_async_remote_copy(src_ref=ref, dst_ref=ref, send_sem=send_x.at[0], recv_sem=sem,
@@ -120,8 +130,8 @@
         for part in parts_of(img):
             src, dst, sem = part_copy(img, me, my_c, part)
             pltpu.make_async_copy(src, dst, sem).start()
-    pltpu.make_async_copy(w1_ref, gw.at[my_z, my_c], recv_w.at[0]).start()
-    pltpu.make_async_copy(ws_ref, gs.at[my_z, my_c], recv_w.at[1]).start()
+    pltpu.make_async_copy(w1_ref, gw.at[my_z, my_c], recv_w.at[0, 1]).start()
+    pltpu.make_async_copy(ws_ref, gs.at[my_z, my_c], recv_w.at[1, 1]).start()
 
     fetches = [pltpu.make_async_copy(src, dst, local.at[k])
                for k, (src, dst) in enumerate(((b1_hbm, b1_ref), (b2_hbm, b2_ref), (w2_hbm, w2_ref)))]
@@ -136,10 +146,17 @@
         send(0, [d, nz - d] if d < nz // 2 else [d], parts_of(0))
         if d < nz // 2:
             pl.semaphore_wait(phase.at[d - 1], 2)
+        if d == 1 and nz >= 8:
+            send_weights([(own, hub) for hub in hubs], 0)
     send(0, [0], parts_of(0))
     near = [d for k in range(1, nz // 2) for d in (k, nz - k)]
     far = [nz // 2] + near[::-1]
-    send_weights(far)
+    if nz >= 8:
+        wait_weights(2, 0)
+        send_weights([(nz - 2, 1), (nz - 2, nz - 1), (2, 1), (2, nz - 1)], 1)
+        send_weights([((2 + (nz - 4) * (1 - my_c)), (nz - 2) - (nz - 4) * (1 - my_c))], 1)
+    else:
+        send_weights([(own, hub) for hub in hubs], 0)
     for img in range(1, last):
         send(img, far + [0], parts_of(img))
 
@@ -153,20 +170,21 @@
         fetch.wait()
     b1c[...] = jnp.broadcast_to(b1_ref[...], (LANES, c_mid)).T
     for t in range(9):
-        w2t[:, t * c_mid:(t + 1) * c_mid] = w2_ref[t // 3, t % 3].astype(jnp.float32).T.astype(w2t.dtype)
+        w2x[:, t * c_mid:(t + 1) * c_mid] = w2_ref[t // 3, t % 3].astype(jnp.float32).T.astype(w2x.dtype)
     wk[...] = jnp.zeros_like(wk)
-    sk[...] = jnp.zeros_like(sk)
 
     def pair(img, p):
-        first_pair(n, height, img, p, xbuf, wt, st, b1c, y1s, sbuf)
+        first_pair(n, height, img, p, xbuf, wt, b1c, y1s)
 
     def second(img, r):
-        y2[img, r] = second_row(r, w2t, b2_ref, y1s, sbuf)
+        y2[img, r] = second_row(img, r, xbuf, w2x, b2_ref, y1s)
 
     def build_weights():
+        wait_weights(nz - 2 if nz >= 8 else 1, 1)
+        if nz < 8:
+            wait_weights(nz - 1, 0)
         shares = []
         for k, ref in enumerate((gw.at[:, my_c], gs.at[:, my_c])):
-            arrived(ref, recv_w.at[k])
             shares.append(pltpu.make_async_remote_copy(
                 src_ref=ref, dst_ref=ref, send_sem=send_v.at[k], recv_sem=recv_v.at[k],
                 device_id={'model': sibling}, device_id_type=MESH))
@@ -182,14 +200,11 @@
                         piece = gw[z, c, dh, dw].astype(jnp.float32)
                         for a in range(2):
                             wk[dw, src, (dh + a) * ch:(dh + a + 1) * ch, a * c_mid:(a + 1) * c_mid] = piece
-                piece = gs[z, c].astype(jnp.float32)
-                for a in range(2):
-                    sk[src, (1 + a) * ch:(2 + a) * ch, a * c_out:(a + 1) * c_out] = piece
 
         loop(0, nz, place)
         for dw in range(3):
             wt[:, dw * kb:(dw + 1) * kb] = wk[dw].reshape(kb, 2 * c_mid).T.astype(wt.dtype)
-        st[...] = sk[...].reshape(kb, 2 * c_out).T.astype(st.dtype)
+        w2x[:, 9 * c_mid:] = gs[...].astype(jnp.float32).reshape(n * ch, c_out).T.astype(w2x.dtype)
 
     def inner_halo(img):
         return pltpu.make_async_remote_copy(
@@ -267,7 +282,7 @@
     arrived(xbuf.at[last, :, pl.ds(0, LATE)], recv_x.at[ni])
 
 
-def finish_kernel(n, height, xbuf, wt, st, w2t, b1c, b2_ref, y1s_in, sbuf_in, y2, out_ref, y1s, sbuf, yb, sem):
+def finish_kernel(n, height, xbuf, wt, w2x, b1c, b2_ref, y1s_in, y2, out_ref, y1s, yb, sem):
     ni, tile = y2.shape[0], y2.shape[1]
     last = ni - 1
     my_c = lax.axis_index('model') % 2
@@ -284,12 +299,11 @@
     step = 3 * b1c.shape[0]
     edge = (1 - my_c) * left + my_c * (tile - left)
     y1s[pl.ds(pl.multiple_of(edge * step, step), 2 * step), :] = y1s_in[pl.ds(pl.multiple_of(edge * step, step), 2 * step), :]
-    sbuf[pl.ds(edge, 2)] = sbuf_in[pl.ds(edge, 2)]
     flip = tile // 2
-    loop(0, first_p, lambda k: first_pair(n, height, last, k + my_c * (flip - 2 * k), xbuf, wt, st, b1c, y1s, sbuf), unroll=2)
+    loop(0, first_p, lambda k: first_pair(n, height, last, k + my_c * (flip - 2 * k), xbuf, wt, b1c, y1s), unroll=2)
 
     def row(k):
-        yb[k] = second_row(k + todo, w2t, b2_ref, y1s, sbuf)
+        yb[k] = second_row(last, k + todo, xbuf, w2x, b2_ref, y1s)
         pltpu.make_async_copy(yb.at[k], out_ref.at[last, k + todo], sem.at[2]).start()
 
     loop(0, left, row, unroll=4)
@@ -311,40 +325,36 @@
         hbm = pl.BlockSpec(memory_space=pltpu.HBM)
         dma = pltpu.SemaphoreType.DMA
         y1s = pltpu.VMEM(((tile + 2) * 3 * c_mid, width), jnp.bfloat16)
-        sbuf = pltpu.VMEM((tile + 2, c_out, width), jnp.float32)
         parts = pl.pallas_call(
             functools.partial(gather_kernel, n),
             out_shape=[
                 pltpu.VMEM((ni, n, tile + 4, halves, ch, LANES), jnp.bfloat16),
                 pltpu.VMEM((2 * c_mid, 3 * kb), jnp.bfloat16),
-                pltpu.VMEM((2 * c_out, kb), jnp.bfloat16),
-                pltpu.VMEM((c_out, 9 * c_mid), jnp.bfloat16),
+                pltpu.VMEM((c_out, 9 * c_mid + n * ch), jnp.bfloat16),
                 pltpu.VMEM((c_mid, LANES), jnp.float32),
                 pltpu.VMEM((1, c_out), jnp.float32),
                 y1s,
-                sbuf,
                 pltpu.VMEM((ni, tile, width, c_out), jnp.float32),
             ],
             in_specs=[hbm] * 6,
-            out_specs=[vmem] * 9,
+            out_specs=[vmem] * 7,
             scratch_shapes=[
                 pltpu.VMEM((nz, 2, 3, 3, ch, c_mid), jnp.bfloat16),
                 pltpu.VMEM((nz, 2, ch, c_out), jnp.bfloat16),
                 pltpu.VMEM((3, n, 4 * ch, 2 * c_mid), jnp.float32),
-                pltpu.VMEM((n, 4 * ch, 2 * c_out), jnp.float32),
                 pltpu.VMEM(w_conv2.shape, w_conv2.dtype),
                 pltpu.VMEM((1, c_mid), jnp.float32),
                 dma((3,)), pltpu.SemaphoreType.REGULAR((nz // 2,)),
-                dma((2,)), dma((ni + 1,)), dma((ni, 2)), dma((ni, 2)), dma((2,)), dma((2,)), dma((2,)), dma((2,)),
+                dma((2,)), dma((ni + 1,)), dma((ni, 2)), dma((ni, 2)), dma((2,)), dma((2, 2)), dma((2,)), dma((2,)),
             ],
             compiler_params=pltpu.CompilerParams(collective_id=0, has_side_effects=True, vmem_limit_bytes=20 * 2**20),
         )(*[pltpu.with_memory_space_constraint(v, pltpu.HBM) for v in (x, w_conv1, b_conv1.reshape(1, c_mid), w_conv2, b_conv2.reshape(1, c_out), w_short)])
         return pl.pallas_call(
             functools.partial(finish_kernel, n, height),
             out_shape=jax.ShapeDtypeStruct((ni, tile, width, c_out), jnp.float32),
-            in_specs=[vmem] * 9,
+            in_specs=[vmem] * 7,
             out_specs=hbm,
-            scratch_shapes=[y1s, sbuf, pltpu.VMEM((LATE + 2, width, c_out), jnp.float32), dma((3,))],
+            scratch_shapes=[y1s, pltpu.VMEM((LATE + 2, width, c_out), jnp.float32), dma((3,))],
             compiler_params=pltpu.CompilerParams(vmem_limit_bytes=20 * 2**20),
         )(*parts)
 

time: 53 us -> 52.7 us (level)
  no operation moved by 1% of the time
where the time goes in v6:
time: 52.7 us; the launch traced here: 52.6 us
  Pallas kernels  52.6 us (100%)
    pallas_call x1, Pallas kernels, local_step(): pl.pallas_call(functools.partial(gather_kernel, n), out_shape=[pltpu.VMEM...  49.4 us
    pallas_call x1, Pallas kernels, local_step(): pl.pallas_call(functools.partial(finish_kernel, n, height), out_shape=jax...  3.27 us

profile of v6, /device:TPU:21, one launch (start us, length us, event | category | flops | bytes accessed | tf_op | source)
XLA Modules:
  0.0 52.6 jit_solution(12277219292906620073)
XLA Ops:
  0.0 49.4 %shard_map.64 = (bf16[3,16,20,2,4,128]{5,4,3,2,1,0:T(4,128)(2,1)S(1)}, bf16[256,768]{1,0:T(8,128)(2,1)S(1)}, bf16[128,1216]{1,0:T(8,128)(2,1)S(1)}, f32[128,128]...) custom-call(bf16[3,256,2,4,128]{4,3,2,1,0:T(4,128)(2,1)} %bitcast.7, ...), custom_call_target="tpu_custom_call" | custom-call | tf_op jit(solution)/shard_map/pallas_call | solution.py:328
  49.4 3.3 %shard_map.65 = f32[3,16,256,128]{3,2,1,0:T(8,128)} custom-call(bf16[3,16,20,2,4,128]{5,4,3,2,1,0:T(4,128)(2,1)S(1)} %get-tuple-element.12.xbuf, bf16[256,768]{1,0:T(8,128)(2,1)S(1)} %get-tuple-element.13.wt, bf16[128,1216]{1,0:T(8,128)(2,1)S(1)} %get-tuple-element.14.w2x, f32[128,128]{1,0:T(8,128)S(1)} %get-tuple-element.15.b1c, ...), custom_call_target="tpu_custom_call" | custom-call | tf_op jit(solution)/shard_map/pallas_call | solution.py:352

commit v7 on v6

--- a/solution.py
+++ b/solution.py
@@ -69,6 +69,7 @@
     tile = height // n
     nz = n // 2
     last = ni - 1
+    assert last == 2
     c_mid, c_out = w1_ref.shape[3], ws_ref.shape[1]
     kb = n * 4 * ch
     me = lax.axis_index('model')
@@ -97,14 +98,18 @@
     def parts_of(img):
         return [(tile, img)] if img < last else [inner, outer]
 
-    def send(img, hops, parts):
-        for part in parts:
-            for d in hops:
-                for c in range(2) if d else (1,):
-                    dest = core(d, c)
-                    src, dst, sem = part_copy(img, dest, (my_c + c) % 2, part)
-                    pltpu.make_async_remote_copy(src_ref=src, dst_ref=dst, send_sem=send_x.at[img // last], recv_sem=sem,
-                                                 device_id={'model': dest}, device_id_type=MESH).start()
+    def send(img, hops, part, batch):
+        for d in hops:
+            for c in range(2) if d else (1,):
+                dest = core(d, c)
+                src, dst, sem = part_copy(img, dest, (my_c + c) % 2, part)
+                pltpu.make_async_remote_copy(src_ref=src, dst_ref=dst, send_sem=send_x.at[batch], recv_sem=sem,
+                                             device_id={'model': dest}, device_id_type=MESH).start()
+
+    def left(batch, copies, rows):
+        ref = xbuf.at[0, pl.ds(0, copies), pl.ds(0, rows)]
+        pltpu.make_async_remote_copy(src_ref=ref, dst_ref=ref, send_sem=send_x.at[batch], recv_sem=recv_x.at[0],
+                                     device_id={'model': sibling}, device_id_type=MESH).wait_send()
 
     hubs = [2, nz - 2] if nz >= 8 else [d for d in range(1, nz)]
 
@@ -143,12 +148,12 @@
         if d < nz // 2:
             for side in (1, nz - 1):
                 pl.semaphore_signal(phase.at[d - 1], inc=1, device_id={'model': core(side, 0)}, device_id_type=MESH)
-        send(0, [d, nz - d] if d < nz // 2 else [d], parts_of(0))
+        send(0, [d, nz - d] if d < nz // 2 else [d], parts_of(0)[0], 0 if d <= nz // 4 else 1)
         if d < nz // 2:
             pl.semaphore_wait(phase.at[d - 1], 2)
         if d == 1 and nz >= 8:
             send_weights([(own, hub) for hub in hubs], 0)
-    send(0, [0], parts_of(0))
+    send(0, [0], parts_of(0)[0], 1)
     near = [d for k in range(1, nz // 2) for d in (k, nz - k)]
     far = [nz // 2] + near[::-1]
     if nz >= 8:
@@ -157,8 +162,10 @@
         send_weights([((2 + (nz - 4) * (1 - my_c)), (nz - 2) - (nz - 4) * (1 - my_c))], 1)
     else:
         send_weights([(own, hub) for hub in hubs], 0)
-    for img in range(1, last):
-        send(img, far + [0], parts_of(img))
+    near_copies = 4 * (nz // 4)
+    first, rest = far[:3], far[3:] + [0]
+    left(0, near_copies, tile)
+    send(1, first, parts_of(1)[0], 2)
 
     for owner, r0 in ((0, 0), (n - 1, tile + 2)):
         @pl.when(me == owner)
@@ -172,6 +179,8 @@
     for t in range(9):
         w2x[:, t * c_mid:(t + 1) * c_mid] = w2_ref[t // 3, t % 3].astype(jnp.float32).T.astype(w2x.dtype)
     wk[...] = jnp.zeros_like(wk)
+    left(1, n - 1 - near_copies, tile)
+    send(1, rest, parts_of(1)[0], 3)
 
     def pair(img, p):
         first_pair(n, height, img, p, xbuf, wt, b1c, y1s)
@@ -235,10 +244,11 @@
     def rows_in(img, lo, hi, unroll):
         loop(lo, hi, lambda k: second(img, k + my_c * (tile - 1 - 2 * k)), unroll=unroll)
 
-    def most(img):
+    def most(img, between):
         loop(1, flip - 1, lambda k: pair_in(img, k), unroll=3)
         inner_halo(img).wait_recv()
         loop(flip - 1, flip + 1, lambda k: pair_in(img, k), unroll=2)
+        between()
         rows_in(img, 2, tile, 7)
 
     def edge(img):
@@ -246,20 +256,25 @@
         pair_in(img, 0)
         rows_in(img, 0, 2, 2)
 
-    for img in range(last):
+    def begin(img):
         arrived(xbuf.at[img, :, pl.ds(0, tile)], recv_x.at[img])
         inner_halo(img).start()
         when(has_outer, lambda: outer_halo(img).start())
-        if img == last - 2:
-            send(last, far + [0], [inner])
-        if img == last - 1:
-            send(last, far + [0], [outer] if last > 1 else [inner, outer])
-        if img == 0:
-            build_weights()
-        else:
-            edge(img - 1)
-        most(img)
-
+
+    begin(0)
+    build_weights()
+    most(0, lambda: None)
+    left(2, 6, tile)
+    send(last, first, inner, 4)
+    begin(1)
+    send(last, rest, inner, 5)
+    edge(0)
+
+    def last_sends():
+        left(4, 6, block - LATE)
+        send(last, far + [0], outer, 6)
+
+    most(1, last_sends)
     arrived(xbuf.at[last, :, pl.ds(0, block - LATE)], recv_x.at[last])
     when(sends_last, lambda: inner_halo(last).start())
     edge(last - 1)
@@ -269,9 +284,9 @@
     loop(flip - 1, flip + 1, lambda k: pair_in(last, k), unroll=2)
     rows_in(last, 2 * first_p, tile, 4)
 
-    for k, sent in enumerate((xbuf.at[pl.ds(0, last), pl.ds(0, n - 1), pl.ds(0, tile)], xbuf.at[last, pl.ds(0, n - 1), pl.ds(0, block)])):
-        pltpu.make_async_remote_copy(src_ref=sent, dst_ref=sent, send_sem=send_x.at[k], recv_sem=recv_x.at[0],
-                                     device_id={'model': sibling}, device_id_type=MESH).wait_send()
+    left(3, n - 7, tile)
+    left(5, n - 7, block - LATE)
+    left(6, n - 1, LATE)
     for k, ref in enumerate((gw.at[pl.ds(0, nz - 1), 0], gs.at[pl.ds(0, nz - 1), 0])):
         pltpu.make_async_remote_copy(src_ref=ref, dst_ref=ref, send_sem=send_w.at[k], recv_sem=recv_w.at[k],
                                      device_id={'model': sibling}, device_id_type=MESH).wait_send()
@@ -345,7 +360,7 @@
                 pltpu.VMEM(w_conv2.shape, w_conv2.dtype),
                 pltpu.VMEM((1, c_mid), jnp.float32),
                 dma((3,)), pltpu.SemaphoreType.REGULAR((nz // 2,)),
-                dma((2,)), dma((ni + 1,)), dma((ni, 2)), dma((ni, 2)), dma((2,)), dma((2, 2)), dma((2,)), dma((2,)),
+                dma((7,)), dma((ni + 1,)), dma((ni, 2)), dma((ni, 2)), dma((2,)), dma((2, 2)), dma((2,)), dma((2,)),
             ],
             compiler_params=pltpu.CompilerParams(collective_id=0, has_side_effects=True, vmem_limit_bytes=20 * 2**20),
         )(*[pltpu.with_memory_space_constraint(v, pltpu.HBM) for v in (x, w_conv1, b_conv1.reshape(1, c_mid), w_conv2, b_conv2.reshape(1, c_out), w_short)])

time: 52.7 us -> 52.4 us (level)
  no operation moved by 1% of the time
where the time goes in v7:
time: 52.4 us; the launch traced here: 52.3 us
  Pallas kernels  52.3 us (100%)
    pallas_call x1, Pallas kernels, local_step(): pl.pallas_call(functools.partial(gather_kernel, n), out_shape=[pltpu.VMEM...  49 us
    pallas_call x1, Pallas kernels, local_step(): pl.pallas_call(functools.partial(finish_kernel, n, height), out_shape=jax...  3.27 us

profile of v7, /device:TPU:21, one launch (start us, length us, event | category | flops | bytes accessed | tf_op | source)
XLA Modules:
  0.0 52.3 jit_solution(18017557466756764159)
XLA Ops:
  0.0 49.0 %shard_map.64 = (bf16[3,16,20,2,4,128]{5,4,3,2,1,0:T(4,128)(2,1)S(1)}, bf16[256,768]{1,0:T(8,128)(2,1)S(1)}, bf16[128,1216]{1,0:T(8,128)(2,1)S(1)}, f32[128,128]...) custom-call(bf16[3,256,2,4,128]{4,3,2,1,0:T(4,128)(2,1)} %bitcast.7, ...), custom_call_target="tpu_custom_call" | custom-call | tf_op jit(solution)/shard_map/pallas_call | solution.py:343
  49.1 3.3 %shard_map.65 = f32[3,16,256,128]{3,2,1,0:T(8,128)} custom-call(bf16[3,16,20,2,4,128]{5,4,3,2,1,0:T(4,128)(2,1)S(1)} %get-tuple-element.12.xbuf, bf16[256,768]{1,0:T(8,128)(2,1)S(1)} %get-tuple-element.13.wt, bf16[128,1216]{1,0:T(8,128)(2,1)S(1)} %get-tuple-element.14.w2x, f32[128,128]{1,0:T(8,128)S(1)} %get-tuple-element.15.b1c, ...), custom_call_target="tpu_custom_call" | custom-call | tf_op jit(solution)/shard_map/pallas_call | solution.py:367

commit v8 on v7

--- a/solution.py
+++ b/solution.py
@@ -9,7 +9,7 @@
 
 MESH = pl.DeviceIdType.MESH
 LANES = 128
-LATE = 6
+LATE = 4
 
 
 def shift_right(v):
@@ -279,10 +279,10 @@
     when(sends_last, lambda: inner_halo(last).start())
     edge(last - 1)
     first_p = LATE // 2 + 1
-    loop(first_p, flip - 1, lambda k: pair_in(last, k), unroll=3)
+    loop(first_p, flip - 1, lambda k: pair_in(last, k), unroll=2)
     when(has_outer, lambda: inner_halo(last).wait_recv())
     loop(flip - 1, flip + 1, lambda k: pair_in(last, k), unroll=2)
-    rows_in(last, 2 * first_p, tile, 4)
+    rows_in(last, 2 * first_p, tile, 5)
 
     left(3, n - 7, tile)
     left(5, n - 7, block - LATE)
@@ -315,13 +315,13 @@
     edge = (1 - my_c) * left + my_c * (tile - left)
     y1s[pl.ds(pl.multiple_of(edge * step, step), 2 * step), :] = y1s_in[pl.ds(pl.multiple_of(edge * step, step), 2 * step), :]
     flip = tile // 2
-    loop(0, first_p, lambda k: first_pair(n, height, last, k + my_c * (flip - 2 * k), xbuf, wt, b1c, y1s), unroll=2)
+    loop(0, first_p, lambda k: first_pair(n, height, last, k + my_c * (flip - 2 * k), xbuf, wt, b1c, y1s), unroll=3)
 
     def row(k):
         yb[k] = second_row(last, k + todo, xbuf, w2x, b2_ref, y1s)
         pltpu.make_async_copy(yb.at[k], out_ref.at[last, k + todo], sem.at[2]).start()
 
-    loop(0, left, row, unroll=4)
+    loop(0, left, row, unroll=3)
     for copy in copies:
         copy.wait()
     pltpu.make_async_copy(yb, out_ref.at[last, pl.ds(todo, left)], sem.at[2]).wait()

time: 52.4 us -> 54.1 us (1.032)
  Pallas kernels: 52.3 us -> 54 us
    pallas_call x1, Pallas kernels: 49 us -> 50.9 us  [local_step(): pl.pallas_call(functools.partial(gather_kernel, n), out_shape=[pltpu.VMEM...]
where the time goes in v8:
time: 54.1 us; the launch traced here: 54 us
  Pallas kernels  54 us (100%)
    pallas_call x1, Pallas kernels, local_step(): pl.pallas_call(functools.partial(gather_kernel, n), out_shape=[pltpu.VMEM...  50.9 us
    pallas_call x1, Pallas kernels, local_step(): pl.pallas_call(functools.partial(finish_kernel, n, height), out_shape=jax...  3.09 us

profile of v8, /device:TPU:21, one launch (start us, length us, event | category | flops | bytes accessed | tf_op | source)
XLA Modules:
  0.0 54.0 jit_solution(14205977656084809062)
XLA Ops:
  0.0 50.9 %shard_map.64 = (bf16[3,16,20,2,4,128]{5,4,3,2,1,0:T(4,128)(2,1)S(1)}, bf16[256,768]{1,0:T(8,128)(2,1)S(1)}, bf16[128,1216]{1,0:T(8,128)(2,1)S(1)}, f32[128,128]...) custom-call(bf16[3,256,2,4,128]{4,3,2,1,0:T(4,128)(2,1)} %bitcast.7, ...), custom_call_target="tpu_custom_call" | custom-call | tf_op jit(solution)/shard_map/pallas_call | solution.py:343
  50.9 3.1 %shard_map.65 = f32[3,16,256,128]{3,2,1,0:T(8,128)} custom-call(bf16[3,16,20,2,4,128]{5,4,3,2,1,0:T(4,128)(2,1)S(1)} %get-tuple-element.12.xbuf, bf16[256,768]{1,0:T(8,128)(2,1)S(1)} %get-tuple-element.13.wt, bf16[128,1216]{1,0:T(8,128)(2,1)S(1)} %get-tuple-element.14.w2x, f32[128,128]{1,0:T(8,128)S(1)} %get-tuple-element.15.b1c, ...), custom_call_target="tpu_custom_call" | custom-call | tf_op jit(solution)/shard_map/pallas_call | solution.py:367

commit v9 on v7

--- a/solution.py
+++ b/solution.py
@@ -272,12 +272,14 @@
 
     def last_sends():
         left(4, 6, block - LATE)
-        send(last, far + [0], outer, 6)
+        send(last, first, outer, 6)
 
     most(1, last_sends)
+    left(5, n - 7, block - LATE)
+    send(last, rest, outer, 7)
+    edge(1)
     arrived(xbuf.at[last, :, pl.ds(0, block - LATE)], recv_x.at[last])
     when(sends_last, lambda: inner_halo(last).start())
-    edge(last - 1)
     first_p = LATE // 2 + 1
     loop(first_p, flip - 1, lambda k: pair_in(last, k), unroll=3)
     when(has_outer, lambda: inner_halo(last).wait_recv())
@@ -285,8 +287,8 @@
     rows_in(last, 2 * first_p, tile, 4)
 
     left(3, n - 7, tile)
-    left(5, n - 7, block - LATE)
-    left(6, n - 1, LATE)
+    left(6, 6, LATE)
+    left(7, n - 7, LATE)
     for k, ref in enumerate((gw.at[pl.ds(0, nz - 1), 0], gs.at[pl.ds(0, nz - 1), 0])):
         pltpu.make_async_remote_copy(src_ref=ref, dst_ref=ref, send_sem=send_w.at[k], recv_sem=recv_w.at[k],
                                      device_id={'model': sibling}, device_id_type=MESH).wait_send()
@@ -360,7 +362,7 @@
                 pltpu.VMEM(w_conv2.shape, w_conv2.dtype),
                 pltpu.VMEM((1, c_mid), jnp.float32),
                 dma((3,)), pltpu.SemaphoreType.REGULAR((nz // 2,)),
-                dma((7,)), dma((ni + 1,)), dma((ni, 2)), dma((ni, 2)), dma((2,)), dma((2, 2)), dma((2,)), dma((2,)),
+                dma((8,)), dma((ni + 1,)), dma((ni, 2)), dma((ni, 2)), dma((2,)), dma((2, 2)), dma((2,)), dma((2,)),
             ],
             compiler_params=pltpu.CompilerParams(collective_id=0, has_side_effects=True, vmem_limit_bytes=20 * 2**20),
         )(*[pltpu.with_memory_space_constraint(v, pltpu.HBM) for v in (x, w_conv1, b_conv1.reshape(1, c_mid), w_conv2, b_conv2.reshape(1, c_out), w_short)])

time: 52.4 us -> 52.4 us (level)
  no operation moved by 1% of the time
where the time goes in v9:
time: 52.4 us; the launch traced here: 52.3 us
  Pallas kernels  52.3 us (100%)
    pallas_call x1, Pallas kernels, local_step(): pl.pallas_call(functools.partial(gather_kernel, n), out_shape=[pltpu.VMEM...  49 us
    pallas_call x1, Pallas kernels, local_step(): pl.pallas_call(functools.partial(finish_kernel, n, height), out_shape=jax...  3.28 us

profile of v9, /device:TPU:21, one launch (start us, length us, event | category | flops | bytes accessed | tf_op | source)
XLA Modules:
  0.0 52.3 jit_solution(18355885623665243042)
XLA Ops:
  0.0 49.0 %shard_map.64 = (bf16[3,16,20,2,4,128]{5,4,3,2,1,0:T(4,128)(2,1)S(1)}, bf16[256,768]{1,0:T(8,128)(2,1)S(1)}, bf16[128,1216]{1,0:T(8,128)(2,1)S(1)}, f32[128,128]...) custom-call(bf16[3,256,2,4,128]{4,3,2,1,0:T(4,128)(2,1)} %bitcast.7, ...), custom_call_target="tpu_custom_call" | custom-call | tf_op jit(solution)/shard_map/pallas_call | solution.py:345
  49.0 3.3 %shard_map.65 = f32[3,16,256,128]{3,2,1,0:T(8,128)} custom-call(bf16[3,16,20,2,4,128]{5,4,3,2,1,0:T(4,128)(2,1)S(1)} %get-tuple-element.12.xbuf, bf16[256,768]{1,0:T(8,128)(2,1)S(1)} %get-tuple-element.13.wt, bf16[128,1216]{1,0:T(8,128)(2,1)S(1)} %get-tuple-element.14.w2x, f32[128,128]{1,0:T(8,128)S(1)} %get-tuple-element.15.b1c, ...), custom_call_target="tpu_custom_call" | custom-call | tf_op jit(solution)/shard_map/pallas_call | solution.py:369

commit v10 on v9

--- a/solution.py
+++ b/solution.py
@@ -284,7 +284,7 @@
     loop(first_p, flip - 1, lambda k: pair_in(last, k), unroll=3)
     when(has_outer, lambda: inner_halo(last).wait_recv())
     loop(flip - 1, flip + 1, lambda k: pair_in(last, k), unroll=2)
-    rows_in(last, 2 * first_p, tile, 4)
+    rows_in(last, 2 * first_p, tile, 8)
 
     left(3, n - 7, tile)
     left(6, 6, LATE)
@@ -323,7 +323,7 @@
         yb[k] = second_row(last, k + todo, xbuf, w2x, b2_ref, y1s)
         pltpu.make_async_copy(yb.at[k], out_ref.at[last, k + todo], sem.at[2]).start()
 
-    loop(0, left, row, unroll=4)
+    loop(0, left, row, unroll=8)
     for copy in copies:
         copy.wait()
     pltpu.make_async_copy(yb, out_ref.at[last, pl.ds(todo, left)], sem.at[2]).wait()

time: 52.4 us -> 51.9 us (level)
  no operation moved by 1% of the time
where the time goes in v10:
time: 51.9 us; the launch traced here: 51.8 us
  Pallas kernels  51.8 us (100%)
    pallas_call x1, Pallas kernels, local_step(): pl.pallas_call(functools.partial(gather_kernel, n), out_shape=[pltpu.VMEM...  48.8 us
    pallas_call x1, Pallas kernels, local_step(): pl.pallas_call(functools.partial(finish_kernel, n, height), out_shape=jax...  3 us

profile of v10, /device:TPU:21, one launch (start us, length us, event | category | flops | bytes accessed | tf_op | source)
XLA Modules:
  0.0 51.8 jit_solution(4549164120072686632)
XLA Ops:
  0.0 48.8 %shard_map.64 = (bf16[3,16,20,2,4,128]{5,4,3,2,1,0:T(4,128)(2,1)S(1)}, bf16[256,768]{1,0:T(8,128)(2,1)S(1)}, bf16[128,1216]{1,0:T(8,128)(2,1)S(1)}, f32[128,128]...) custom-call(bf16[3,256,2,4,128]{4,3,2,1,0:T(4,128)(2,1)} %bitcast.7, ...), custom_call_target="tpu_custom_call" | custom-call | tf_op jit(solution)/shard_map/pallas_call | solution.py:345
  48.8 3.0 %shard_map.65 = f32[3,16,256,128]{3,2,1,0:T(8,128)} custom-call(bf16[3,16,20,2,4,128]{5,4,3,2,1,0:T(4,128)(2,1)S(1)} %get-tuple-element.12.xbuf, bf16[256,768]{1,0:T(8,128)(2,1)S(1)} %get-tuple-element.13.wt, bf16[128,1216]{1,0:T(8,128)(2,1)S(1)} %get-tuple-element.14.w2x, f32[128,128]{1,0:T(8,128)S(1)} %get-tuple-element.15.b1c, ...), custom_call_target="tpu_custom_call" | custom-call | tf_op jit(solution)/shard_map/pallas_call | solution.py:369

commit v11 on v10

--- a/solution.py
+++ b/solution.py
@@ -263,9 +263,11 @@
 
     begin(0)
     build_weights()
-    most(0, lambda: None)
-    left(2, 6, tile)
-    send(last, first, inner, 4)
+    def inner_sends():
+        left(2, 6, tile)
+        send(last, first, inner, 4)
+
+    most(0, inner_sends)
     begin(1)
     send(last, rest, inner, 5)
     edge(0)

time: 51.9 us -> 52.8 us (1.017)
  Pallas kernels: 51.8 us -> 52.7 us
    pallas_call x1, Pallas kernels: 48.8 us -> 49.7 us  [local_step(): pl.pallas_call(functools.partial(gather_kernel, n), out_shape=[pltpu.VMEM...]
where the time goes in v11:
time: 52.8 us; the launch traced here: 52.7 us
  Pallas kernels  52.7 us (100%)
    pallas_call x1, Pallas kernels, local_step(): pl.pallas_call(functools.partial(gather_kernel, n), out_shape=[pltpu.VMEM...  49.7 us
    pallas_call x1, Pallas kernels, local_step(): pl.pallas_call(functools.partial(finish_kernel, n, height), out_shape=jax...  3.01 us

profile of v11, /device:TPU:21, one launch (start us, length us, event | category | flops | bytes accessed | tf_op | source)
XLA Modules:
  0.0 52.7 jit_solution(18143817747564501081)
XLA Ops:
  0.0 49.7 %shard_map.64 = (bf16[3,16,20,2,4,128]{5,4,3,2,1,0:T(4,128)(2,1)S(1)}, bf16[256,768]{1,0:T(8,128)(2,1)S(1)}, bf16[128,1216]{1,0:T(8,128)(2,1)S(1)}, f32[128,128]...) custom-call(bf16[3,256,2,4,128]{4,3,2,1,0:T(4,128)(2,1)} %bitcast.7, ...), custom_call_target="tpu_custom_call" | custom-call | tf_op jit(solution)/shard_map/pallas_call | solution.py:347
  49.7 3.0 %shard_map.65 = f32[3,16,256,128]{3,2,1,0:T(8,128)} custom-call(bf16[3,16,20,2,4,128]{5,4,3,2,1,0:T(4,128)(2,1)S(1)} %get-tuple-element.12.xbuf, bf16[256,768]{1,0:T(8,128)(2,1)S(1)} %get-tuple-element.13.wt, bf16[128,1216]{1,0:T(8,128)(2,1)S(1)} %get-tuple-element.14.w2x, f32[128,128]{1,0:T(8,128)S(1)} %get-tuple-element.15.b1c, ...), custom_call_target="tpu_custom_call" | custom-call | tf_op jit(solution)/shard_map/pallas_call | solution.py:371

commit v12 on v10

--- a/solution.py
+++ b/solution.py
@@ -165,7 +165,7 @@
     near_copies = 4 * (nz // 4)
     first, rest = far[:3], far[3:] + [0]
     left(0, near_copies, tile)
-    send(1, first, parts_of(1)[0], 2)
+    send(1, first[:1], parts_of(1)[0], 2)
 
     for owner, r0 in ((0, 0), (n - 1, tile + 2)):
         @pl.when(me == owner)
@@ -180,6 +180,7 @@
         w2x[:, t * c_mid:(t + 1) * c_mid] = w2_ref[t // 3, t % 3].astype(jnp.float32).T.astype(w2x.dtype)
     wk[...] = jnp.zeros_like(wk)
     left(1, n - 1 - near_copies, tile)
+    send(1, first[1:], parts_of(1)[0], 2)
     send(1, rest, parts_of(1)[0], 3)
 
     def pair(img, p):

time: 51.9 us -> 52.7 us (1.015)
  Pallas kernels: 51.8 us -> 52.6 us
    pallas_call x1, Pallas kernels: 48.8 us -> 49.6 us  [local_step(): pl.pallas_call(functools.partial(gather_kernel, n), out_shape=[pltpu.VMEM...]
where the time goes in v12:
time: 52.7 us; the launch traced here: 52.6 us
  Pallas kernels  52.6 us (100%)
    pallas_call x1, Pallas kernels, local_step(): pl.pallas_call(functools.partial(gather_kernel, n), out_shape=[pltpu.VMEM...  49.6 us
    pallas_call x1, Pallas kernels, local_step(): pl.pallas_call(functools.partial(finish_kernel, n, height), out_shape=jax...  2.99 us

profile of v12, /device:TPU:21, one launch (start us, length us, event | category | flops | bytes accessed | tf_op | source)
XLA Modules:
  0.0 52.6 jit_solution(2536764759359875346)
XLA Ops:
  0.0 49.6 %shard_map.64 = (bf16[3,16,20,2,4,128]{5,4,3,2,1,0:T(4,128)(2,1)S(1)}, bf16[256,768]{1,0:T(8,128)(2,1)S(1)}, bf16[128,1216]{1,0:T(8,128)(2,1)S(1)}, f32[128,128]...) custom-call(bf16[3,256,2,4,128]{4,3,2,1,0:T(4,128)(2,1)} %bitcast.7, ...), custom_call_target="tpu_custom_call" | custom-call | tf_op jit(solution)/shard_map/pallas_call | solution.py:346
  49.7 3.0 %shard_map.65 = f32[3,16,256,128]{3,2,1,0:T(8,128)} custom-call(bf16[3,16,20,2,4,128]{5,4,3,2,1,0:T(4,128)(2,1)S(1)} %get-tuple-element.12.xbuf, bf16[256,768]{1,0:T(8,128)(2,1)S(1)} %get-tuple-element.13.wt, bf16[128,1216]{1,0:T(8,128)(2,1)S(1)} %get-tuple-element.14.w2x, f32[128,128]{1,0:T(8,128)S(1)} %get-tuple-element.15.b1c, ...), custom_call_target="tpu_custom_call" | custom-call | tf_op jit(solution)/shard_map/pallas_call | solution.py:370

commit v13 on v10

--- a/solution.py
+++ b/solution.py
@@ -273,10 +273,9 @@
     def last_sends():
         left(4, 6, block - LATE)
         send(last, first, outer, 6)
+        send(last, rest, outer, 7)
 
     most(1, last_sends)
-    left(5, n - 7, block - LATE)
-    send(last, rest, outer, 7)
     edge(1)
     arrived(xbuf.at[last, :, pl.ds(0, block - LATE)], recv_x.at[last])
     when(sends_last, lambda: inner_halo(last).start())
@@ -287,6 +286,7 @@
     rows_in(last, 2 * first_p, tile, 8)
 
     left(3, n - 7, tile)
+    left(5, n - 7, block - LATE)
     left(6, 6, LATE)
     left(7, n - 7, LATE)
     for k, ref in enumerate((gw.at[pl.ds(0, nz - 1), 0], gs.at[pl.ds(0, nz - 1), 0])):

time: 51.9 us -> 51.2 us (0.987)
  Pallas kernels: 51.8 us -> 51.1 us
    pallas_call x1, Pallas kernels: 48.8 us -> 48.1 us  [local_step(): pl.pallas_call(functools.partial(gather_kernel, n), out_shape=[pltpu.VMEM...]
where the time goes in v13:
time: 51.2 us; the launch traced here: 51.1 us
  Pallas kernels  51.1 us (100%)
    pallas_call x1, Pallas kernels, local_step(): pl.pallas_call(functools.partial(gather_kernel, n), out_shape=[pltpu.VMEM...  48.1 us
    pallas_call x1, Pallas kernels, local_step(): pl.pallas_call(functools.partial(finish_kernel, n, height), out_shape=jax...  3 us

profile of v13, /device:TPU:21, one launch (start us, length us, event | category | flops | bytes accessed | tf_op | source)
XLA Modules:
  0.0 51.1 jit_solution(5549981098551864362)
XLA Ops:
  0.0 48.1 %shard_map.64 = (bf16[3,16,20,2,4,128]{5,4,3,2,1,0:T(4,128)(2,1)S(1)}, bf16[256,768]{1,0:T(8,128)(2,1)S(1)}, bf16[128,1216]{1,0:T(8,128)(2,1)S(1)}, f32[128,128]...) custom-call(bf16[3,256,2,4,128]{4,3,2,1,0:T(4,128)(2,1)} %bitcast.7, ...), custom_call_target="tpu_custom_call" | custom-call | tf_op jit(solution)/shard_map/pallas_call | solution.py:345
  48.1 3.0 %shard_map.65 = f32[3,16,256,128]{3,2,1,0:T(8,128)} custom-call(bf16[3,16,20,2,4,128]{5,4,3,2,1,0:T(4,128)(2,1)S(1)} %get-tuple-element.12.xbuf, bf16[256,768]{1,0:T(8,128)(2,1)S(1)} %get-tuple-element.13.wt, bf16[128,1216]{1,0:T(8,128)(2,1)S(1)} %get-tuple-element.14.w2x, f32[128,128]{1,0:T(8,128)S(1)} %get-tuple-element.15.b1c, ...), custom_call_target="tpu_custom_call" | custom-call | tf_op jit(solution)/shard_map/pallas_call | solution.py:369
